TPU v7x, 32 devices: a whole 2x2x4 slice. The times are simulated.
32 devices in a mesh: blk: 16 (over z, y, core), tgt: 2 (over x).
Axes of the slice: x: 2, y: 2, z: 4, core: 2. Of those that a mesh axis runs over, the one named last changes fastest.
Arguments:
- history: float32 [32768, 1536], P(('blk', 'tgt')), may hold values from 0 to 2
- weights: bfloat16 [16, 2048, 32768], P(None, 'tgt', 'blk'), may hold values from -0.03125 to 0.03125
- delays: int32 [8, 8], replicated, may hold values from 16 to 64
- area_blocks: int32 [8], replicated, may hold values from 1 to 3, 16 in all
- potential: float32 [24, 32768], P(None, ('blk', 'tgt')), may hold values from -6 to 6
- leak: float32 [32768], P(('blk', 'tgt')), may hold values from 0.03 to 0.6
- drive: float32 [32768], P(('blk', 'tgt')), may hold values from -6 to 6
Outputs:
- rate_steps: float32 [16, 24, 32768], P(None, None, ('blk', 'tgt'))
- last_potential: float32 [24, 32768], P(None, ('blk', 'tgt'))
Inputs may be any that keep to these rules, and one draw needn't show every extreme that they name: Area a consists of area_blocks[a] consecutive blocks of 2048 neurons; areas follow one another in order.
All inputs are finite; a program needn't handle non-finite values.
Results may differ from a plain program's by a relative error of at most 0.00083.
Values may be sent and summed in bfloat16 or wider, within the bound.
No kernel may reach another device: no remote copies, remote signals or barrier semaphores. Data moves between devices by JAX's collectives and lax.ppermute only.
A program may use at most 192 MiB of HBM per device.

v0:
```python
import jax
import jax.numpy as jnp
from jax import lax
from jax.sharding import PartitionSpec as P

STEPS = 16


def block_areas(area_blocks, block_count):
    boundary = jnp.cumsum(area_blocks)
    blocks = jnp.arange(block_count, dtype=jnp.int32)
    return jnp.sum((boundary[None, :] <= blocks[:, None]).astype(jnp.int32), axis=1)


def on_device(history, weights, delays, area_blocks, potential, leak, drive):
    block_count = weights.shape[0]
    piece_width = weights.shape[1]
    columns = history.shape[1]
    trial_count = potential.shape[0]
    window_width = STEPS * trial_count
    area_of_block = block_areas(area_blocks, block_count)
    my_block = lax.axis_index("blk")
    my_area = area_of_block[my_block]
    history_low = history.astype(jnp.bfloat16)

    def window(lag_step, column):
        start = columns - lag_step * trial_count
        return lax.dynamic_slice_in_dim(column, start, window_width, 1)

    lag_steps = delays[my_area][area_of_block]
    arrived = lax.all_gather(history_low, "blk", axis=0, tiled=True)
    shard_count = arrived.shape[0] // piece_width
    shaped = arrived.reshape(shard_count, piece_width, columns)
    delayed_input = jax.vmap(window, in_axes=(0, 0))(lag_steps, shaped)
    partial_input = jnp.einsum(
        "gyw,gyt->wt", delayed_input, weights, preferred_element_type=jnp.float32
    )
    own_input = lax.psum_scatter(partial_input, "tgt", scatter_dimension=1, tiled=True)
    own_input = own_input.reshape(STEPS, trial_count, piece_width)

    def advance(membrane_state, synaptic):
        membrane_state = membrane_state + leak * (drive - membrane_state + synaptic)
        return (membrane_state, jax.nn.softplus(membrane_state))

    last_potential, rate_steps = lax.scan(advance, potential, own_input)
    return (rate_steps, last_potential)


def solution(mesh):
    in_specs = (
        P(("blk", "tgt"), None),
        P(None, "tgt", "blk"),
        P(),
        P(),
        P(None, ("blk", "tgt")),
        P(("blk", "tgt")),
        P(("blk", "tgt")),
    )
    out_specs = (P(None, None, ("blk", "tgt")), P(None, ("blk", "tgt")))
    return jax.shard_map(
        on_device, mesh=mesh, in_specs=in_specs, out_specs=out_specs, check_vma=False
    )
```

profile of v0, /device:TPU:0, one launch (start us, length us, event | category | flops | bytes accessed | tf_op | source)
XLA Modules:
  0.0 444.1 jit_solution(3117740394669187895)
XLA Ops:
  7.2 4.8 %convert_element_type.6 = bf16[1024,1536]{1,0:T(8,128)(2,1)} convert(f32[1024,1536]{1,0:T(8,128)} %param.9) | non-fusion elementwise | flops 1572864 | bytes 9437184 | tf_op jit(solution)/shard_map/convert_element_type | solution.py:24
  15.4 246.6 %all-gather.2.cloned.1.call-done = bf16[16384,1536]{1,0:T(8,128)(2,1)} async-done(((bf16[1024,1536]{1,0:T(8,128)(2,1)}), bf16[16384,1536]{1,0:T(8,128)(2,1)}) %all-gather.2.cloned.1.call-update) | async-done | bytes 50331664 | tf_op jit(solution)/shard_map/all_gather | solution.py:31
  262.0 68.1 %while.14 = (s32[]{:T(128)}, bf16[16,1024,1536]{2,1,0:T(8,128)(2,1)}, s32[16,3]{0,1:T(4,128)S(1)}, bf16[16,1024,384]{2,1,0:T(8,128)(2,1)}, s32[]{:T(128)}) while((s32[]{:T(128)}, bf16[16,1024,1536]{2,1,0:T(8,128)(2,1)}, s32[16,3]{0,1:T(4,128)S(1)}, bf16[16,1024,384]{2,1,0:T(8,128)(2,1)}, s32[]{:T(128)}) %tuple.50), condition=%wide.while_cond, body=%wide.while_body.sunk | while | flops 2 | bytes 1574505 | solution.py:28
  262.6 3.6 dynamic-slice_dynamic-update-slice_fusion.2
  266.8 3.6 dynamic-slice_dynamic-update-slice_fusion.2
  271.1 3.6 dynamic-slice_dynamic-update-slice_fusion.2
  275.3 3.6 dynamic-slice_dynamic-update-slice_fusion.2
  279.6 3.7 dynamic-slice_dynamic-update-slice_fusion.2
  283.8 3.7 dynamic-slice_dynamic-update-slice_fusion.2
  288.1 3.7 dynamic-slice_dynamic-update-slice_fusion.2
  292.4 3.6 dynamic-slice_dynamic-update-slice_fusion.2
  296.6 3.7 dynamic-slice_dynamic-update-slice_fusion.2
  300.9 3.6 dynamic-slice_dynamic-update-slice_fusion.2
  305.2 3.7 dynamic-slice_dynamic-update-slice_fusion.2
  309.5 3.6 dynamic-slice_dynamic-update-slice_fusion.2
  313.7 3.7 dynamic-slice_dynamic-update-slice_fusion.2
  318.0 3.6 dynamic-slice_dynamic-update-slice_fusion.2
  322.3 3.6 dynamic-slice_dynamic-update-slice_fusion.2
  326.5 3.6 dynamic-slice_dynamic-update-slice_fusion.2
  330.2 37.1 %convolution_bitcast_fusion = f32[384,2048]{1,0:T(8,128)} fusion(bf16[16,1024,384]{2,1,0:T(8,128)(2,1)} %get-tuple-element.44, bf16[16,1024,2048]{2,1,0:T(8,128)(2,1)} %param.10), kind=kOutput, calls=%fused_computation.9 | convolution fusion | flops 25769803776 | bytes 82837504 | tf_op jit(solution)/shard_map/gyw,gyt->wt/dot_general | solution.py:35
  367.3 43.6 %reduce-scatter.2.cloned.1.call-done = f32[384,1024]{1,0:T(8,128)} async-done(((f32[384,2048]{1,0:T(8,128)}), f32[384,1024]{1,0:T(8,128)}) %reduce-scatter.2.cloned.1.call-update) | async-done | bytes 1572880 | tf_op jit(solution)/shard_map/reduce_scatter | solution.py:38
  410.8 25.8 %while.13 = (s32[]{:T(128)}, f32[24,1024]{1,0:T(8,128)S(1)}, f32[16,24,1024]{2,1,0:T(8,128)}, f32[1024]{0:T(1024)S(1)}, f32[1024]{0:T(1024)S(1)}, /*index=5*/f32[16,24,1024]{2,1,0:T(8,128)}, s32[]{:T(128)}) while((s32[]{:T(128)}, f32[24,1024]{1,0:T(8,128)S(1)}, f32[16,24,1024]{2,1,0:T(8,128)}, f32[1024]{0:T(1024)S(1)}, f32[1024]{0:T(1024)S(1)}, ...), condition=%wide.region_4.5_spmd, body=%wide.region_3.4_spmd.sunk | while | flops 245762 | bytes 401997 | solution.py:45
  410.8 1.6 fusion.11
  414.1 1.6 fusion.11
  (76 shorter events, 34.6 us)
Async XLA Ops:
  7.2 7.5 %copy-start = (s32[8,8]{1,0:T(8,128)S(1)}, s32[8,8]{1,0:T(8,128)}, u32[]{:S(2)}) copy-start(s32[8,8]{1,0:T(8,128)} %param.11) | copy-start | bytes 772
  7.2 4.9 %copy-start.6 = (s32[8]{0:T(128)S(1)}, s32[8]{0:T(128)}, u32[]{:S(2)}) copy-start(s32[8]{0:T(128)} %param.12) | copy-start | bytes 100
  7.2 254.8 %all-gather.2.cloned.1.call-start = ((), (), s32[]{:S(2)}) async-start(), calls=%async_computation.1 | async-start | bytes 53477376 | tf_op jit(solution)/shard_map/all_gather | solution.py:31
  12.1 398.8 %reduce-scatter.2.cloned.1.call-start = ((), (), s32[]{:S(2)}) async-start(), calls=%async_computation.2 | async-start | bytes 4718592 | tf_op jit(solution)/shard_map/reduce_scatter | solution.py:38
  330.1 80.7 %copy-start.3 = (f32[24,1024]{1,0:T(8,128)S(1)}, f32[24,1024]{1,0:T(8,128)}, u32[]{:S(2)}) copy-start(f32[24,1024]{1,0:T(8,128)} %param.13) | copy-start | bytes 294916
  330.1 80.7 %copy-start.4 = (f32[1024]{0:T(1024)S(1)}, f32[1024]{0:T(1024)}, u32[]{:S(2)}) copy-start(f32[1024]{0:T(1024)} %param.14) | copy-start | bytes 12292
  330.1 80.7 %copy-start.5 = (f32[1024]{0:T(1024)S(1)}, f32[1024]{0:T(1024)}, u32[]{:S(2)}) copy-start(f32[1024]{0:T(1024)} %param.15) | copy-start | bytes 12292
  330.1 107.1 %copy-start.1 = (s32[8,8]{1,0:T(8,128)S(1)}, s32[8,8]{1,0:T(8,128)}, u32[]{:S(2)}) copy-start(s32[8,8]{1,0:T(8,128)} %param.11) | copy-start | bytes 772
  436.6 0.6 copy-start.2
Sparse Core Ops, SparseCore 0:
  12.2 249.7 all-gather.1
  367.4 43.3 reduce-scatter.1
where the time goes:
time: 446 us; the launch traced here: 444 us
  waiting for transfers between devices  290 us (65%)
  local copies, waits for them, and re-layouts  70 us (16%)
  matrix products  37.1 us (8%)
  other arithmetic  30.9 us (7%)
  between operations  15.8 us (4%)
    all_gather x1, waiting for transfers between devices, on_device(): arrived = lax.all_gather(history_low, 'blk', axis=0, tiled=True)  247 us
    gather x48, local copies, waits for them, and re-layouts  68.1 us
    reduce_scatter x1, waiting for transfers between devices, on_device(): lax.psum_scatter(partial_input, 'tgt', scatter_dimension=1, tiled=True)  43.6 us
    dot_general x1, matrix products, on_device(): jnp.einsum('gyw,gyt->wt', delayed_input, weights, preferred_element_type=...  37.1 us
    dynamic_update_slice x16, other arithmetic, on_device(): last_potential, rate_steps = lax.scan(advance, potential, own_input)  25.8 us
  transfers between devices with their start and end apart: 2, of which 2 were waited for; matrix products, arithmetic and copies ran while one was open for 0% of the time, Pallas kernels for 0%

commit v1 on v0

v1 whole, which is shorter than its diff:
```python
import functools
import jax
import jax.numpy as jnp
from jax import lax
from jax.experimental import pallas as pl
from jax.experimental.pallas import tpu as pltpu
from jax.sharding import PartitionSpec as P

STEPS = 16
CHUNKS = 2
GROUP = 4
FORCE = None
SUB = 8


def turn(history, chunks):
    rows, columns = history.shape
    width = rows // chunks
    tile = 384 if columns % 384 == 0 else columns

    def kernel(x_ref, *out_refs):
        for k, out_ref in enumerate(out_refs):
            out_ref[...] = x_ref[k * width : (k + 1) * width, :].T.astype(jnp.bfloat16)

    return pl.pallas_call(
        kernel,
        grid=(columns // tile,),
        in_specs=[pl.BlockSpec((rows, tile), lambda i: (0, i))],
        out_specs=[pl.BlockSpec((tile, width), lambda i: (i, 0))] * chunks,
        out_shape=[jax.ShapeDtypeStruct((columns, width), jnp.bfloat16)] * chunks,
        name="turn",
    )(history)


def gain(starts, arrived, weights, chunk, depth, shares, total=None, split=None):
    blocks, _, _, width = arrived.shape
    targets = weights.shape[2]
    share = targets // shares
    length = depth // SUB
    given = total is not None

    def kernel(start_ref, *refs):
        old_ref = refs[0] if given else None
        a_ref, w_ref, *out_refs = refs[1 if given else 0 : -1]
        sum_ref = refs[-1]
        i = pl.program_id(0)
        product = jnp.dot(a_ref[0].reshape(depth, width), w_ref[0], preferred_element_type=jnp.float32)

        @pl.when(i == 0)
        def _():
            sum_ref[...] = product + old_ref[...] if given else product

        @pl.when(i > 0)
        def _():
            sum_ref[...] += product

        @pl.when(i == blocks - 1)
        def _():
            if split is None:
                out_refs[0][...] = sum_ref[...]
            else:
                for k in range(shares):
                    for out_ref in out_refs:
                        out_ref[k] = sum_ref[:, k * share : (k + 1) * share].astype(out_ref.dtype)

    whole = pl.BlockSpec((depth, targets), lambda i, s: (0, 0))
    if split is None:
        outs = [jax.ShapeDtypeStruct((depth, targets), jnp.float32)]
        out_specs = [whole]
    else:
        outs = [jax.ShapeDtypeStruct((shares, depth, share), t) for t in split]
        out_specs = [pl.BlockSpec((shares, depth, share), lambda i, s: (0, 0, 0))] * len(split)
    return pl.pallas_call(
        kernel,
        grid_spec=pltpu.PrefetchScalarGridSpec(
            num_scalar_prefetch=1,
            grid=(blocks,),
            in_specs=([whole] if given else [])
            + [
                pl.BlockSpec(
                    (pl.Element(1), pl.Element(length), pl.Element(SUB), pl.Element(width)),
                    lambda i, s: (i, s[i], 0, 0),
                ),
                pl.BlockSpec((1, width, targets), lambda i, s: (i, chunk, 0)),
            ],
            out_specs=out_specs,
            scratch_shapes=[pltpu.VMEM((depth, targets), jnp.float32)],
        ),
        out_shape=outs,
        cost_estimate=pl.CostEstimate(
            flops=2 * depth * width * blocks * targets,
            bytes_accessed=2 * width * blocks * (targets + depth),
            transcendentals=0,
        ),
        name="gain",
    )(starts, *([total] if given else []), arrived, weights)


def advance(share_at, own, arrived, potential, leak, drive):
    trials, share = potential.shape
    steps = own[0].shape[1]

    def kernel(at_ref, *refs):
        own_refs, in_refs = refs[: len(own)], refs[len(own) : len(own) + len(arrived)]
        potential_ref, leak_ref, drive_ref, rate_ref, last_ref = refs[-5:]
        membrane = potential_ref[...]
        leak_row, drive_row = leak_ref[...], drive_ref[...]
        for s in range(steps):
            synaptic = own_refs[0][0, s]
            for ref in own_refs[1:]:
                synaptic += ref[0, s]
            for ref in in_refs:
                synaptic += ref[s].astype(jnp.float32)
            membrane = membrane + leak_row * (drive_row - membrane + synaptic)
            rate_ref[s] = jnp.maximum(membrane, 0.0) + jnp.log1p(jnp.exp(-jnp.abs(membrane)))
        last_ref[...] = membrane

    tile = 256 if share % 256 == 0 else share
    wide = pl.BlockSpec((steps, trials, tile), lambda i, a: (0, 0, i))
    flat = pl.BlockSpec((trials, tile), lambda i, a: (0, i))
    line = pl.BlockSpec((1, tile), lambda i, a: (0, i))
    mine = pl.BlockSpec((1, steps, trials, tile), lambda i, a: (a[0], 0, 0, i))
    return pl.pallas_call(
        kernel,
        grid_spec=pltpu.PrefetchScalarGridSpec(
            num_scalar_prefetch=1,
            grid=(share // tile,),
            in_specs=[mine] * len(own) + [wide] * len(arrived) + [flat, line, line],
            out_specs=[wide, flat],
        ),
        out_shape=[
            jax.ShapeDtypeStruct((steps, trials, share), jnp.float32),
            jax.ShapeDtypeStruct(potential.shape, jnp.float32),
        ],
        name="advance",
    )(share_at[None], *own, *arrived, potential, leak[None], drive[None])


def collect(table, inputs, sizes, cases, length, chosen=None):
    width = inputs[0].shape[2]

    def kernel(table_ref, *refs):
        in_refs, out_refs, sems = refs[: len(inputs)], refs[len(inputs) : -1], refs[-1]

        def carry_out(case):
            copies = [
                pltpu.make_async_copy(
                    in_refs[a].at[pl.ds(table_ref[entry], length)],
                    out_refs[o].at[pl.ds(place * length, length)],
                    sems.at[n],
                )
                for n, (a, entry, o, place) in enumerate(case)
            ]
            for copy in copies:
                copy.start()
            for copy in copies:
                copy.wait()

        if chosen is None:
            carry_out(cases[0])
        else:
            for n, case in enumerate(cases):
                pl.when(table_ref[chosen] == n)(functools.partial(carry_out, case))

    outs = [jax.ShapeDtypeStruct((n * length, SUB, width), jnp.bfloat16) for n in sizes]
    return pl.pallas_call(
        kernel,
        grid_spec=pltpu.PrefetchScalarGridSpec(
            num_scalar_prefetch=1,
            grid=(1,),
            in_specs=[pl.BlockSpec(memory_space=pltpu.MemorySpace.HBM)] * len(inputs),
            out_specs=[pl.BlockSpec(o.shape, lambda i, t: (0, 0, 0)) for o in outs],
            scratch_shapes=[pltpu.SemaphoreType.DMA((max(len(c) for c in cases),))],
        ),
        out_shape=outs,
        cost_estimate=pl.CostEstimate(flops=3 * 10**9, bytes_accessed=6 << 20, transcendentals=0),
        name="collect",
    )(table, *inputs)


def gain_group(table, entry, windows, weights, halves, depth, shares, total=None, part=None, kind=jnp.float32):
    width = windows[0].shape[2]
    targets = weights.shape[2]
    share = targets // shares
    tile = 512 if share % 512 == 0 else share
    tiles = share // tile
    length = depth // SUB
    given = total is not None

    def kernel(table_ref, *refs):
        old_ref = refs[0] if given else None
        refs = refs[1 if given else 0 :]
        a_refs, w_refs, out_ref = refs[:GROUP], refs[GROUP:-1], refs[-1]
        value = old_ref[0] if given else None
        for n in range(len(halves)):
            for j in range(GROUP):
                a = a_refs[j][n * length : (n + 1) * length].reshape(depth, width)
                product = jnp.dot(a, w_refs[n * GROUP + j][0], preferred_element_type=jnp.float32)
                value = product if value is None else value + product
        out_ref[0] = value.astype(out_ref.dtype)

    def share_of(i, t):
        return i // tiles if part is None else lax.rem(t[AT_SHARE] + part, shares)

    def weight_at(half, j):
        return lambda i, t: (t[entry + j], half, share_of(i, t) * tiles + i % tiles)

    parts = shares if part is None else 1
    return pl.pallas_call(
        kernel,
        grid_spec=pltpu.PrefetchScalarGridSpec(
            num_scalar_prefetch=1,
            grid=(parts * tiles,),
            in_specs=([pl.BlockSpec((1, depth, tile), lambda i, t: (share_of(i, t), 0, i % tiles))] if given else [])
            + [pl.BlockSpec(w.shape, lambda i, t: (0, 0, 0)) for w in windows]
            + [pl.BlockSpec((1, width, tile), weight_at(h, j)) for h in halves for j in range(GROUP)],
            out_specs=pl.BlockSpec((1, depth, tile), lambda i, t: (i // tiles, 0, i % tiles)),
        ),
        out_shape=jax.ShapeDtypeStruct((parts, depth, share), kind),
        cost_estimate=pl.CostEstimate(
            flops=2 * depth * width * len(halves) * GROUP * parts * share, bytes_accessed=16 << 20, transcendentals=0
        ),
        name="gain_group",
    )(table, *([total] if given else []), *windows, *([weights] * (GROUP * len(halves))))


LINE = 4
ORDER = ((1, 2, 3), (0, 2, 3), (3, 1, 0), (2, 1, 0))
CASE = ((3, 3, 3), (0, 1, 1), (1, 0, 0), (2, 2, 2))
FORWARDS = ((0, 1), (0, -1), (1, 1), (1, -1), (2, 1), (2, -1))


def at_window(o, j):
    return o * GROUP + j


def at_slot(f, k):
    return LINE * GROUP + f * GROUP + k


AT_CASE = LINE * GROUP + len(FORWARDS) * GROUP
AT_BLOCK = AT_CASE + LINE
AT_SHARE = AT_BLOCK + LINE * GROUP
AT_COUNT = AT_SHARE + 1
ENTRIES = AT_COUNT + 1


def plan(area_blocks, delays, place, hist, per):
    areas = area_blocks.shape[0]
    blocks = LINE * GROUP
    length = STEPS * per

    def kernel(sizes_ref, delays_ref, place_ref, out_ref, area_ref):
        for b in range(blocks):
            edge, area = jnp.int32(0), jnp.int32(0)
            for a in range(areas):
                edge = edge + sizes_ref[a]
                area = area + (edge <= b).astype(jnp.int32)
            area_ref[b] = jnp.minimum(area, areas - 1)
        group, member = place_ref[0], place_ref[1]

        def of_group(values):
            picked = jnp.int32(values[0])
            for g in range(1, LINE):
                picked = jnp.where(group == g, values[g], picked)
            return picked

        def start(target_area, source_group):
            return (hist - delays_ref[target_area, area_ref[source_group * GROUP + member]]) * per

        mine = area_ref[group * GROUP]
        for o in range(LINE):
            source = group if o == 0 else of_group([r[o - 1] for r in ORDER])
            case = jnp.int32(0) if o == 0 else of_group([r[o - 1] for r in CASE])
            out_ref[AT_CASE + o] = case
            for j in range(GROUP):
                peer = area_ref[group * GROUP + (member ^ j)]
                out_ref[at_window(o, j)] = jnp.where(case >= 2, (peer - mine) * length, start(peer, source))
                out_ref[AT_BLOCK + o * GROUP + j] = source * GROUP + (member ^ j)
        for f, (made, d) in enumerate(FORWARDS):
            beyond = jnp.clip(group + d, 0, LINE - 1) * GROUP
            source = jnp.clip(group - made * d, 0, LINE - 1)
            for k in range(GROUP):
                area = jnp.minimum(area_ref[beyond] + k, area_ref[beyond + GROUP - 1])
                out_ref[at_slot(f, k)] = start(area, source)
        out_ref[AT_SHARE] = place_ref[2]
        outer = [area_ref[g * GROUP + GROUP - 1] - area_ref[g * GROUP] for g in (0, LINE - 1)]
        out_ref[AT_COUNT] = jnp.maximum(outer[0], outer[1])

    smem = pl.BlockSpec(memory_space=pltpu.MemorySpace.SMEM)
    return pl.pallas_call(
        kernel,
        in_specs=[smem] * 3,
        out_specs=smem,
        out_shape=jax.ShapeDtypeStruct((ENTRIES,), jnp.int32),
        scratch_shapes=[pltpu.SMEM((blocks,), jnp.int32)],
        name="plan",
    )(area_blocks, delays, place)


def line_of_groups(slot_count, table, turned, weights, potential, leak, drive, *, size, shares):
    targets = weights.shape[2]
    trials = potential.shape[0]
    per = trials // SUB
    length = STEPS * per
    depth = STEPS * trials
    share = targets // shares
    last = LINE - 1

    def hop(x, s, d, outer):
        pairs = []
        for g in range(LINE):
            to = g + d
            if 0 <= to <= last and 0 <= to - s * d <= last and (to == (last if d == 1 else 0)) == outer:
                pairs += [(g * GROUP + m, to * GROUP + m) for m in range(GROUP)]
        return lax.ppermute(x, "blk", pairs)

    def swap(windows):
        given = [windows[0]]
        for j in range(1, GROUP):
            given.append(lax.ppermute(windows[j], "blk", [(b, b ^ j) for b in range(size)]))
        return given

    def tie(later, earlier):
        return lax.optimization_barrier((later, earlier))[0]

    ab = range(2)
    counts = [slot_count] * 2
    full, slots = {}, {}
    last_step = []

    def gather(inputs, sizes, cases, chosen=None):
        inputs = tie(inputs, last_step) if last_step else inputs
        outs = collect(table, inputs, sizes, cases, length, chosen)
        last_step[:] = outs
        return outs

    def forward(s, h):
        if s == 2:
            for d in (1, -1):
                full[s, d, h] = hop(full[s - 1, d, h], s, d, False)
        outs = gather(
            [full[s - 1, 1, h], full[s - 1, -1, h]], counts,
            [[(f, at_slot(2 * (s - 1) + f, k), f, k) for f in ab for k in range(slot_count)]],
        )
        for f, d in enumerate((1, -1)):
            slots[s, d, h] = hop(outs[f], s, d, True)

    def windows_of(o, halves):
        inner = {1: (1, 1), 2: (1, 1), 3: (2, 2)}[o]
        buffers = [full[inner[0], 1, h] for h in halves] + [full[inner[1], -1, h] for h in halves]
        buffers += [slots[o, 1, h] for h in halves] + [slots[o, -1, h] for h in halves]
        n = len(halves)
        cases = [
            [(c * n + h, at_window(o, j), j, h) for j in range(GROUP) for h in range(n)] for c in range(4)
        ]
        return swap(gather(buffers, [n] * GROUP, cases, AT_CASE + o))

    def add(o, windows, halves, total=None, part=None, kind=jnp.float32):
        windows = [tie(windows[0], last_step)] + windows[1:]
        return gain_group(
            table, AT_BLOCK + o * GROUP, windows, weights, halves, depth, shares, total, part, kind
        )

    share_at = table[AT_SHARE]
    shape = (STEPS, trials, share)
    came = []

    def send(part, k):
        came.append(lax.ppermute(part, "tgt", [(t, (t + k) % shares) for t in range(shares)]).reshape(shape))

    outs = gather(
        turned, counts * 2, [[(h, at_slot(f, k), 2 * h + f, k) for h in ab for f in ab for k in range(slot_count)]]
    )
    for h in ab:
        for f, d in enumerate((1, -1)):
            slots[1, d, h] = hop(outs[2 * h + f], 1, d, True)
            full[1, d, h] = hop(turned[h], 1, d, False)
    own = gather(turned, [2] * GROUP, [[(h, at_window(0, j), j, h) for j in range(GROUP) for h in ab]])
    own = swap(own)
    forward(2, 0)
    first = windows_of(1, ab)
    forward(2, 1)
    total = add(0, own, ab)
    forward(3, 0)
    second = windows_of(2, ab)
    early = add(1, first, ab, total)
    for k in range(1, shares):
        send(lax.dynamic_index_in_dim(early, (share_at + k) % shares, 0, False), k)
    forward(3, 1)
    third = [windows_of(3, (0,))]
    third += [windows_of(3, (1,))]
    late = add(2, second, ab)
    late = add(3, third[0], (0,), late)
    for k in range(1, shares):
        send(add(3, third[1], (1,), late, k, jnp.bfloat16), k)
    late = add(3, third[1], (1,), late, 0)
    return advance(
        share_at, [early.reshape((shares,) + shape)], came + [late.reshape(shape)], potential, leak, drive
    )


def gather_all(history, weights, delays, boundary, potential, leak, drive, *, size, shares, spread):
    block_count, piece, targets = weights.shape
    trials = potential.shape[0]
    hist = history.shape[1] // trials
    per = trials // SUB
    depth = STEPS * trials
    chunks = max(1, min(CHUNKS, piece // 128))
    width = piece // chunks
    share = targets // shares
    blocks = jnp.arange(block_count, dtype=jnp.int32)
    area = jnp.sum((boundary[None, :] <= blocks[:, None]).astype(jnp.int32), axis=1)
    my_area = area[lax.axis_index("blk")]
    share_at = lax.axis_index("tgt")
    starts = ((hist - delays[my_area][area]) * per).astype(jnp.int32)

    turned = turn(history, chunks)
    arrived = [
        lax.all_gather(t, "blk", axis=0, tiled=False).reshape(size, hist * per, SUB, width) for t in turned
    ]
    own, came, total = [], [], None
    for c in range(chunks):
        if c < chunks - 2:
            (total,) = gain(starts, arrived[c], weights, c, depth, shares, total)
        elif c == chunks - 2:
            (early,) = gain(starts, arrived[c], weights, c, depth, shares, total, (jnp.float32,))
            own.append(early.reshape(shares, STEPS, trials, share))
            came += spread(early)
        else:
            late, late_low = gain(
                starts, arrived[c], weights, c, depth, shares, None, (jnp.float32, jnp.bfloat16 if chunks > 1 else jnp.float32)
            )
            own.append(late.reshape(shares, STEPS, trials, share))
            came += spread(late_low)
    return advance(share_at, own, came, potential, leak, drive)


def on_device(history, weights, delays, area_blocks, potential, leak, drive, *, size, shares):
    _, piece, targets = weights.shape
    trials = potential.shape[0]
    share = targets // shares
    boundary = jnp.cumsum(area_blocks)
    share_at = lax.axis_index("tgt")

    def spread(sums):
        came = []
        for k in range(1, shares):
            part = lax.dynamic_index_in_dim(sums, (share_at + k) % shares, 0, False)
            part = lax.ppermute(part, "tgt", [(t, (t + k) % shares) for t in range(shares)])
            came.append(part.reshape(STEPS, trials, share))
        return came

    if size != LINE * GROUP or piece % 256:
        return tuple(
            gather_all(history, weights, delays, boundary, potential, leak, drive, size=size, shares=shares, spread=spread)
        )
    me = lax.axis_index("blk")
    per = trials // SUB
    place = jnp.stack([me // GROUP, me % GROUP, share_at])
    table = plan(area_blocks, delays, place, history.shape[1] // trials, per)
    history = lax.optimization_barrier((history, table))[0]
    turned = [t.reshape(-1, SUB, piece // 2) for t in turn(history, 2)]
    line = functools.partial(line_of_groups, size=size, shares=shares)
    rest = (table, turned, weights, potential, leak, drive)
    if FORCE is not None:
        return tuple(line(FORCE, *rest))

    def branch(count):
        def run(*rest):
            return line(count, *rest)

        return run

    branches = [branch(count) for count in range(3, GROUP + 1)]
    return tuple(lax.switch(jnp.clip(table[AT_COUNT] - 2, 0, GROUP - 3), branches, *rest))


def solution(mesh):
    in_specs = (
        P(("blk", "tgt"), None),
        P(None, "tgt", "blk"),
        P(),
        P(),
        P(None, ("blk", "tgt")),
        P(("blk", "tgt")),
        P(("blk", "tgt")),
    )
    out_specs = (P(None, None, ("blk", "tgt")), P(None, ("blk", "tgt")))
    return jax.shard_map(
        functools.partial(on_device, size=mesh.shape["blk"], shares=mesh.shape["tgt"]),
        mesh=mesh, in_specs=in_specs, out_specs=out_specs, check_vma=False,
    )
```

time: 446 us -> 325 us (0.73)
  waiting for transfers between devices: 290 us -> 156 us
  Pallas kernels: 0 us -> 113 us
  local copies, waits for them, and re-layouts: 70 us -> 3.38 us
  starting transfers between devices: 0.08 us -> 46.7 us
  matrix products: 37.1 us -> 0 us
  other arithmetic: 30.9 us -> 0.6 us
  between operations: 15.8 us -> 1.32 us
    all_gather x1 -> x0, waiting for transfers between devices: 247 us -> none  [on_device(): arrived = lax.all_gather(history_low, 'blk', axis=0, tiled=True)]
    ppermute x0 -> x37, waiting for transfers between devices: none -> 156 us  [the longest x20 114 us: hop(): return lax.ppermute(x, 'blk', pairs)]
    pallas_call x0 -> x19, Pallas kernels: none -> 113 us  [the longest x6 61.3 us: gain_group(): pl.pallas_call(kernel, grid_spec=pltpu.PrefetchScalarGridSpec(num_scalar_...]
    gather x49 -> x0, local copies, waits for them, and re-layouts: 68.8 us -> none
    ppermute x0 -> x37, starting transfers between devices: none -> 46.7 us  [the longest x20 34.9 us: hop(): return lax.ppermute(x, 'blk', pairs)]
    reduce_scatter x1 -> x0, waiting for transfers between devices: 43.6 us -> none  [on_device(): lax.psum_scatter(partial_input, 'tgt', scatter_dimension=1, tiled=True)]
    dot_general x1 -> x0, matrix products: 37.1 us -> none  [on_device(): jnp.einsum('gyw,gyt->wt', delayed_input, weights, preferred_element_type=...]
    dynamic_update_slice x16 -> x0, other arithmetic: 25.8 us -> none  [on_device(): last_potential, rate_steps = lax.scan(advance, potential, own_input)]
  transfers between devices with their start and end apart: 2 -> 37, of which waited for: 2 -> 12; matrix products, arithmetic and copies ran while one was open for 0% -> 1% of each run, Pallas kernels for 0% -> 31%
where the time goes in v1:
time: 325 us; the launch traced here: 322 us
  waiting for transfers between devices  156 us (48%)
  Pallas kernels  113 us (35%)
  starting transfers between devices  46.7 us (14%)
  local copies, waits for them, and re-layouts  3.38 us (1%)
    ppermute x20, waiting for transfers between devices, hop(): return lax.ppermute(x, 'blk', pairs)  114 us
    pallas_call x6, Pallas kernels, gain_group(): pl.pallas_call(kernel, grid_spec=pltpu.PrefetchScalarGridSpec(num_scalar_...  61.3 us
    pallas_call x10, Pallas kernels, collect(): pl.pallas_call(kernel, grid_spec=pltpu.PrefetchScalarGridSpec(num_scalar_...  39.3 us
    ppermute x20, starting transfers between devices, hop(): return lax.ppermute(x, 'blk', pairs)  34.9 us
    ppermute x15, waiting for transfers between devices, swap(): lax.ppermute(windows[j], 'blk', [(b, b ^ j) for b in range(size)])  29.3 us
    ppermute x2, waiting for transfers between devices, send(): lax.ppermute(part, 'tgt', [(t, (t + k) % shares) for t in range(shares)])  12.9 us
    ppermute x15, starting transfers between devices, swap(): lax.ppermute(windows[j], 'blk', [(b, b ^ j) for b in range(size)])  8.77 us
  transfers between devices with their start and end apart: 37, of which 12 were waited for; matrix products, arithmetic and copies ran while one was open for 1% of the time, Pallas kernels for 31%

profile of v1, /device:TPU:0, one launch (start us, length us, event | category | flops | bytes accessed | tf_op | source)
XLA Modules:
  0.0 321.9 jit_solution(14826057628347937324)
XLA Ops:
  4.2 5.2 %turn.1 = (bf16[1536,512]{1,0:T(8,128)(2,1)}, bf16[1536,512]{1,0:T(8,128)(2,1)}) custom-call(f32[1024,1536]{1,0:T(8,128)} %x_ref), custom_call_target="tpu_custom_call" | custom-call | tf_op jit(solution)/shard_map/turn/pallas_call | solution.py:25
  9.4 312.5 %conditional.1 = ((f32[16,24,1024]{2,1,0:T(8,128)}, f32[24,1024]{1,0:T(8,128)})) conditional(s32[]{:T(128)} %bitcast.19, (s32[62]{0:T(128)S(1)}, bf16[192,8,512]{2,1,0:T(8,128)(2,1)}, bf16[192,8,512]{2,1,0:T(8,128)(2,1)}, bf16[16,1024,2048]{2,1,0:T(8,128)(2,1)}, f32[1024]{0:T(1024)}, /*index=5*/f32[1024]{0:T(1024)}, f32[24,1024]{1,0:T(8,128)}) %tuple.43, ...), branch_computations={%region_0.1_spmd, %region_1.2_spmd} | conditional | flops 55769808896 | bytes 392071008 | solution.py:476
  9.4 5.0 %collective-permute-start.2 = (bf16[192,8,512]{2,1,0:T(8,128)(2,1)}, bf16[192,8,512]{2,1,0:T(8,128)(2,1)S(1)}, u32[]{:S(2)}, u32[]{:S(2)}) collective-permute-start(bf16[192,8,512]{2,1,0:T(8,128)(2,1)} %get-tuple-element.35.refs_0_), channel_id=1, source_target_pairs={{0,8},{2,10},{4,12},{6,14},{8,16},{10,18},{12,20},{14,22},{1,9},{3... | collective-permute-start | bytes 4718600 | tf_op jit(solution)/shard_map/cond/branch_0_fun/ppermute | solution.py:316
  15.2 5.6 %collect.20 = (bf16[144,8,512]{2,1,0:T(8,128)(2,1)}, bf16[144,8,512]{2,1,0:T(8,128)(2,1)}, bf16[144,8,512]{2,1,0:T(8,128)(2,1)}, bf16[144,8,512]{2,1,0:T(8,128)(2,1)}) custom-call(s32[62]{0:T(128)S(1)} %get-tuple-element.28.table_ref, bf16[192,8,512]{2,1,0:T(8,128)(2,1)} %get-tuple-element.35.refs_0_, bf16[192,8,512]{2,1,0:T(8,128)(2,1)} %get-tuple-element.36.refs_1_), custom_call_target="tpu_custom_call" | custom-call | flops 3000000000 | bytes 6291456 | tf_op jit(solution)/shard_map/cond/branch_0_fun/collect/pallas_call | solution.py:166
  21.6 5.0 %collective-permute-start = (bf16[192,8,512]{2,1,0:T(8,128)(2,1)}, bf16[192,8,512]{2,1,0:T(8,128)(2,1)}, u32[]{:S(2)}, u32[]{:S(2)}) collective-permute-start(bf16[192,8,512]{2,1,0:T(8,128)(2,1)} %get-tuple-element.36.refs_1_), channel_id=1, source_target_pairs={{0,8},{2,10},{4,12},{6,14},{8,16},{10,18},{12,20},{14,22},{1,9},{3... | collective-permute-start | bytes 4718600 | tf_op jit(solution)/shard_map/cond/branch_0_fun/ppermute | solution.py:316
  30.0 19.4 %collective-permute-done.2.refs_0_ = bf16[192,8,512]{2,1,0:T(8,128)(2,1)S(1)} collective-permute-done((bf16[192,8,512]{2,1,0:T(8,128)(2,1)}, bf16[192,8,512]{2,1,0:T(8,128)(2,1)S(1)}, u32[]{:S(2)}, u32[]{:S(2)}) %collective-permute-start.2) | collective-permute-done | bytes 1572896 | tf_op jit(solution)/shard_map/cond/branch_0_fun/ppermute | solution.py:316
  52.1 4.3 %collect.21 = (bf16[96,8,512]{2,1,0:T(8,128)(2,1)}, bf16[96,8,512]{2,1,0:T(8,128)(2,1)}, bf16[96,8,512]{2,1,0:T(8,128)(2,1)}, bf16[96,8,512]{2,1,0:T(8,128)(2,1)}) custom-call(s32[62]{0:T(128)S(1)} %get-tuple-element.28.table_ref, bf16[192,8,512]{2,1,0:T(8,128)(2,1)} %get-tuple-element.35.refs_0_, bf16[192,8,512]{2,1,0:T(8,128)(2,1)} %get-tuple-element.36.refs_1_), custom_call_target="tpu_custom_call" | custom-call | flops 3000000000 | bytes 6291456 | tf_op jit(solution)/shard_map/cond/branch_0_fun/collect/pallas_call | solution.py:166
  60.1 20.4 %collective-permute-done.6.refs_6_ = bf16[144,8,512]{2,1,0:T(8,128)(2,1)} collective-permute-done((bf16[144,8,512]{2,1,0:T(8,128)(2,1)}, bf16[144,8,512]{2,1,0:T(8,128)(2,1)}, u32[]{:S(2)}, u32[]{:S(2)}) %collective-permute-start.6) | collective-permute-done | bytes 1179680 | tf_op jit(solution)/shard_map/cond/branch_0_fun/ppermute | solution.py:316
  82.1 20.5 %collective-permute-done.7.refs_7_ = bf16[144,8,512]{2,1,0:T(8,128)(2,1)} collective-permute-done((bf16[144,8,512]{2,1,0:T(8,128)(2,1)}, bf16[144,8,512]{2,1,0:T(8,128)(2,1)}, u32[]{:S(2)}, u32[]{:S(2)}) %collective-permute-start.7) | collective-permute-done | bytes 1179680 | tf_op jit(solution)/shard_map/cond/branch_0_fun/ppermute | solution.py:316
  104.6 4.1 %collect.23 = (bf16[96,8,512]{2,1,0:T(8,128)(2,1)}, bf16[96,8,512]{2,1,0:T(8,128)(2,1)}, bf16[96,8,512]{2,1,0:T(8,128)(2,1)}, bf16[96,8,512]{2,1,0:T(8,128)(2,1)}) custom-call(s32[62]{0:T(128)S(1)} %get-tuple-element.28.table_ref, bf16[192,8,512]{2,1,0:T(8,128)(2,1)} %copy-done.23, bf16[192,8,512]{2,1,0:T(8,128)(2,1)} %collective-permute-done.refs_1_.refs_0_, ...), custom_call_target="tpu_custom_call" | custom-call | flops 3000000000 | bytes 6291456 | tf_op jit(solution)/shard_map/cond/branch_0_fun/collect/pallas_call | solution.py:166
  115.4 14.4 %collective-permute-done.9.refs_2_ = bf16[96,8,512]{2,1,0:T(8,128)(2,1)S(1)} collective-permute-done((bf16[96,8,512]{2,1,0:T(8,128)(2,1)}, bf16[96,8,512]{2,1,0:T(8,128)(2,1)S(1)}, u32[]{:S(2)}, u32[]{:S(2)}) %collective-permute-start.9) | collective-permute-done | bytes 786464 | tf_op jit(solution)/shard_map/cond/branch_0_fun/ppermute | solution.py:321
  136.2 28.2 %collective-permute-done.13.refs_6_ = bf16[144,8,512]{2,1,0:T(8,128)(2,1)S(1)} collective-permute-done((bf16[144,8,512]{2,1,0:T(8,128)(2,1)}, bf16[144,8,512]{2,1,0:T(8,128)(2,1)S(1)}, u32[]{:S(2)}, u32[]{:S(2)}) %collective-permute-start.13) | collective-permute-done | bytes 1179680 | tf_op jit(solution)/shard_map/cond/branch_0_fun/ppermute | solution.py:316
  164.4 20.6 %collective-permute-done.14.refs_7_ = bf16[144,8,512]{2,1,0:T(8,128)(2,1)} collective-permute-done((bf16[144,8,512]{2,1,0:T(8,128)(2,1)}, bf16[144,8,512]{2,1,0:T(8,128)(2,1)}, u32[]{:S(2)}, u32[]{:S(2)}) %collective-permute-start.14) | collective-permute-done | bytes 1179680 | tf_op jit(solution)/shard_map/cond/branch_0_fun/ppermute | solution.py:316
  194.4 4.2 %collect.26 = (bf16[96,8,512]{2,1,0:T(8,128)(2,1)}, bf16[96,8,512]{2,1,0:T(8,128)(2,1)}, bf16[96,8,512]{2,1,0:T(8,128)(2,1)}, bf16[96,8,512]{2,1,0:T(8,128)(2,1)}) custom-call(s32[62]{0:T(128)S(1)} %get-tuple-element.28.table_ref, bf16[192,8,512]{2,1,0:T(8,128)(2,1)} %copy-done.23, bf16[192,8,512]{2,1,0:T(8,128)(2,1)} %collective-permute-done.refs_1_.refs_0_, ...), custom_call_target="tpu_custom_call" | custom-call | flops 3000000000 | bytes 6291456 | tf_op jit(solution)/shard_map/cond/branch_0_fun/collect/pallas_call | solution.py:166
  205.4 13.2 %gain_group.12.refs_0_ = f32[2,384,1024]{2,1,0:T(8,128)} custom-call(s32[62]{0:T(128)S(1)} %get-tuple-element.28.table_ref, bf16[96,8,512]{2,1,0:T(8,128)(2,1)} %get-tuple-element.61.refs_0_, bf16[96,8,512]{2,1,0:T(8,128)(2,1)} %copy-done.6, bf16[96,8,512]{2,1,0:T(8,128)(2,1)} %copy-done.7, bf16[96,8,512]{2,1,0:T(8,128)(2,1)} %collective-permute-done.10.refs_3_, ...), custom_call_target="tpu_custom_call" | custom-call | flops 6442450944 | bytes 16777216 | tf_op jit(solution)/shard_map/cond/branch_0_fun/gain_group/pallas_call | solution.py:209
  222.9 13.3 %gain_group.13 = f32[2,384,1024]{2,1,0:T(8,128)} custom-call(s32[62]{0:T(128)S(1)} %get-tuple-element.28.table_ref, f32[2,384,1024]{2,1,0:T(8,128)} %gain_group.12.refs_0_, bf16[96,8,512]{2,1,0:T(8,128)(2,1)} %get-tuple-element.79.refs_1_, bf16[96,8,512]{2,1,0:T(8,128)(2,1)} %copy-done.8, bf16[96,8,512]{2,1,0:T(8,128)(2,1)} %copy-done.9, ...), custom_call_target="tpu_custom_call" | custom-call | flops 6442450944 | bytes 16777216 | tf_op jit(solution)/shard_map/cond/branch_0_fun/gain_group/pallas_call | solution.py:209
  248.7 7.4 %collective-permute-done.29.refs_3_ = bf16[96,8,512]{2,1,0:T(8,128)(2,1)} collective-permute-done((bf16[96,8,512]{2,1,0:T(8,128)(2,1)}, bf16[96,8,512]{2,1,0:T(8,128)(2,1)}, u32[]{:S(2)}, u32[]{:S(2)}) %collective-permute-start.29) | collective-permute-done | bytes 786464 | tf_op jit(solution)/shard_map/cond/branch_0_fun/ppermute | solution.py:321
  258.7 6.7 %collective-permute-done.31.refs_3_ = bf16[48,8,512]{2,1,0:T(8,128)(2,1)} collective-permute-done((bf16[48,8,512]{2,1,0:T(8,128)(2,1)}, bf16[48,8,512]{2,1,0:T(8,128)(2,1)}, u32[]{:S(2)}, u32[]{:S(2)}) %collective-permute-start.31) | collective-permute-done | bytes 393248 | tf_op jit(solution)/shard_map/cond/branch_0_fun/ppermute | solution.py:321
  265.4 13.2 %gain_group.14.refs_0_ = f32[2,384,1024]{2,1,0:T(8,128)} custom-call(s32[62]{0:T(128)S(1)} %get-tuple-element.28.table_ref, bf16[96,8,512]{2,1,0:T(8,128)(2,1)} %get-tuple-element.100.refs_0_, bf16[96,8,512]{2,1,0:T(8,128)(2,1)} %collective-permute-done.27.refs_1_, bf16[96,8,512]{2,1,0:T(8,128)(2,1)} %collective-permute-done.28.refs_2_, ...), custom_call_target="tpu_custom_call" | custom-call | flops 6442450944 | bytes 16777216 | tf_op jit(solution)/shard_map/cond/branch_0_fun/gain_group/pallas_call | solution.py:209
  278.6 9.5 %gain_group.15.refs_0_ = f32[2,384,1024]{2,1,0:T(8,128)} custom-call(s32[62]{0:T(128)S(1)} %get-tuple-element.28.table_ref, f32[2,384,1024]{2,1,0:T(8,128)} %gain_group.14.refs_0_, bf16[48,8,512]{2,1,0:T(8,128)(2,1)} %get-tuple-element.101.refs_1_, bf16[48,8,512]{2,1,0:T(8,128)(2,1)} %copy-done.15, bf16[48,8,512]{2,1,0:T(8,128)(2,1)} %collective-permute-done.31.refs_3_, ...), custom_call_target="tpu_custom_call" | custom-call | flops 3221225472 | bytes 16777216 | tf_op jit(solution)/shard_map/cond/branch_0_fun/gain_group/pallas_call | solution.py:209
  288.9 6.0 %gain_group.16 = bf16[1,384,1024]{2,1,0:T(8,128)(2,1)} custom-call(s32[62]{0:T(128)S(1)} %get-tuple-element.28.table_ref, f32[2,384,1024]{2,1,0:T(8,128)} %gain_group.15.refs_0_, bf16[48,8,512]{2,1,0:T(8,128)(2,1)} %get-tuple-element.102.refs_1_, bf16[48,8,512]{2,1,0:T(8,128)(2,1)} %collective-permute-done.33.refs_2_, ...), custom_call_target="tpu_custom_call" | custom-call | flops 1610612736 | bytes 16777216 | tf_op jit(solution)/shard_map/cond/branch_0_fun/gain_group/pallas_call | solution.py:209
  296.5 6.1 %gain_group.17 = f32[1,384,1024]{2,1,0:T(8,128)} custom-call(s32[62]{0:T(128)S(1)} %get-tuple-element.28.table_ref, f32[2,384,1024]{2,1,0:T(8,128)} %gain_group.15.refs_0_, bf16[48,8,512]{2,1,0:T(8,128)(2,1)} %get-tuple-element.102.refs_1_, bf16[48,8,512]{2,1,0:T(8,128)(2,1)} %collective-permute-done.33.refs_2_, ...), custom_call_target="tpu_custom_call" | custom-call | flops 1610612736 | bytes 16777216 | tf_op jit(solution)/shard_map/cond/branch_0_fun/gain_group/pallas_call | solution.py:209
  302.6 12.9 %collective-permute-done.36 = bf16[1,384,1024]{2,1,0:T(8,128)(2,1)S(1)} collective-permute-done((bf16[1,384,1024]{2,1,0:T(8,128)(2,1)}, bf16[1,384,1024]{2,1,0:T(8,128)(2,1)S(1)}, u32[]{:S(2)}, u32[]{:S(2)}) %collective-permute-start.36) | collective-permute-done | bytes 786464 | tf_op jit(solution)/shard_map/cond/branch_0_fun/ppermute | solution.py:370
  316.4 5.4 %advance.2 = (f32[16,24,1024]{2,1,0:T(8,128)}, f32[24,1024]{1,0:T(8,128)}) custom-call(s32[1]{0:T(128)} %slice.6.at_ref, f32[2,16,24,1024]{3,2,1,0:T(8,128)} %bitcast.24, f32[16,24,1024]{2,1,0:T(8,128)} %bitcast.3.refs_1_, bf16[16,24,1024]{2,1,0:T(8,128)(2,1)} %bitcast.28, f32[16,24,1024]{2,1,0:T(8,128)} %bitcast.26, f32[24,1024]{1,0:T(8,128)S(1)} %copy-done.17, ...), custom_call_target="tpu_custom_call" | custom-call | tf_op jit(solution)/shard_map/cond/branch_0_fun/advance/pallas_call | solution.py:123
  (108 shorter events, 68.9 us)
Async XLA Ops:
  9.4 40.0 %collective-permute-start.2 = (bf16[192,8,512]{2,1,0:T(8,128)(2,1)}, bf16[192,8,512]{2,1,0:T(8,128)(2,1)S(1)}, u32[]{:S(2)}, u32[]{:S(2)}) collective-permute-start(bf16[192,8,512]{2,1,0:T(8,128)(2,1)} %get-tuple-element.35.refs_0_), channel_id=1, source_target_pairs={{0,8},{2,10},{4,12},{6,14},{8,16},{10,18},{12,20},{14,22},{1,9},{3... | collective-permute-start | bytes 4718600 | tf_op jit(solution)/shard_map/cond/branch_0_fun/ppermute | solution.py:316
  14.5 36.3 %collective-permute-start.3 = (bf16[192,8,512]{2,1,0:T(8,128)(2,1)}, bf16[192,8,512]{2,1,0:T(8,128)(2,1)S(1)}, u32[]{:S(2)}, u32[]{:S(2)}) collective-permute-start(bf16[192,8,512]{2,1,0:T(8,128)(2,1)} %get-tuple-element.35.refs_0_), channel_id=1, source_target_pairs={{16,8},{18,10},{20,12},{22,14},{24,16},{26,18},{28,20},{30,22},{17... | collective-permute-start | bytes 4718600 | tf_op jit(solution)/shard_map/cond/branch_0_fun/ppermute | solution.py:316
  21.6 81.1 %collective-permute-start = (bf16[192,8,512]{2,1,0:T(8,128)(2,1)}, bf16[192,8,512]{2,1,0:T(8,128)(2,1)}, u32[]{:S(2)}, u32[]{:S(2)}) collective-permute-start(bf16[192,8,512]{2,1,0:T(8,128)(2,1)} %get-tuple-element.36.refs_1_), channel_id=1, source_target_pairs={{0,8},{2,10},{4,12},{6,14},{8,16},{10,18},{12,20},{14,22},{1,9},{3... | collective-permute-start | bytes 4718600 | tf_op jit(solution)/shard_map/cond/branch_0_fun/ppermute | solution.py:316
  26.5 76.1 %collective-permute-start.1 = (bf16[192,8,512]{2,1,0:T(8,128)(2,1)}, bf16[192,8,512]{2,1,0:T(8,128)(2,1)}, u32[]{:S(2)}, u32[]{:S(2)}) collective-permute-start(bf16[192,8,512]{2,1,0:T(8,128)(2,1)} %get-tuple-element.36.refs_1_), channel_id=1, source_target_pairs={{16,8},{18,10},{20,12},{22,14},{24,16},{26,18},{28,20},{30,22},{17... | collective-permute-start | bytes 4718600 | tf_op jit(solution)/shard_map/cond/branch_0_fun/ppermute | solution.py:316
  28.4 31.6 %collective-permute-start.5 = (bf16[144,8,512]{2,1,0:T(8,128)(2,1)}, bf16[144,8,512]{2,1,0:T(8,128)(2,1)}, u32[]{:S(2)}, u32[]{:S(2)}) collective-permute-start(bf16[144,8,512]{2,1,0:T(8,128)(2,1)} %get-tuple-element.33), channel_id=1, source_target_pairs={{16,24},{18,26},{20,28},{22,30},{17,25},{19,27},{21,29},{23,31}} | collective-permute-start | bytes 3538952 | tf_op jit(solution)/shard_map/cond/branch_0_fun/ppermute | solution.py:316
  49.4 31.0 %collective-permute-start.6 = (bf16[144,8,512]{2,1,0:T(8,128)(2,1)}, bf16[144,8,512]{2,1,0:T(8,128)(2,1)}, u32[]{:S(2)}, u32[]{:S(2)}) collective-permute-start(bf16[144,8,512]{2,1,0:T(8,128)(2,1)} %get-tuple-element.32), channel_id=1, source_target_pairs={{8,0},{10,2},{12,4},{14,6},{9,1},{11,3},{13,5},{15,7}} | collective-permute-start | bytes 3538952 | tf_op jit(solution)/shard_map/cond/branch_0_fun/ppermute | solution.py:316
  50.8 51.9 %collective-permute-start.7 = (bf16[144,8,512]{2,1,0:T(8,128)(2,1)}, bf16[144,8,512]{2,1,0:T(8,128)(2,1)}, u32[]{:S(2)}, u32[]{:S(2)}) collective-permute-start(bf16[144,8,512]{2,1,0:T(8,128)(2,1)} %get-tuple-element.34), channel_id=1, source_target_pairs={{8,0},{10,2},{12,4},{14,6},{9,1},{11,3},{13,5},{15,7}} | collective-permute-start | bytes 3538952 | tf_op jit(solution)/shard_map/cond/branch_0_fun/ppermute | solution.py:316
  60.0 54.7 %collective-permute-start.8 = (bf16[96,8,512]{2,1,0:T(8,128)(2,1)}, bf16[96,8,512]{2,1,0:T(8,128)(2,1)S(1)}, u32[]{:S(2)}, u32[]{:S(2)}) collective-permute-start(bf16[96,8,512]{2,1,0:T(8,128)(2,1)} %get-tuple-element.38), channel_id=1, source_target_pairs={{0,2},{2,0},{4,6},{6,4},{8,10},{10,8},{12,14},{14,12},{16,18},{18,... | collective-permute-start | bytes 2359304 | tf_op jit(solution)/shard_map/cond/branch_0_fun/ppermute | solution.py:321
  80.5 51.1 %collective-permute-start.11 = (bf16[144,8,512]{2,1,0:T(8,128)(2,1)}, bf16[144,8,512]{2,1,0:T(8,128)(2,1)}, u32[]{:S(2)}, u32[]{:S(2)}) collective-permute-start(bf16[144,8,512]{2,1,0:T(8,128)(2,1)} %get-tuple-element.43), channel_id=1, source_target_pairs={{16,24},{18,26},{20,28},{22,30},{17,25},{19,27},{21,29},{23,31}} | collective-permute-start | bytes 3538952 | tf_op jit(solution)/shard_map/cond/branch_0_fun/ppermute | solution.py:316
  102.7 32.1 %collective-permute-start.15 = (bf16[192,8,512]{2,1,0:T(8,128)(2,1)S(1)}, bf16[192,8,512]{2,1,0:T(8,128)(2,1)}, u32[]{:S(2)}, u32[]{:S(2)}) collective-permute-start(bf16[192,8,512]{2,1,0:T(8,128)(2,1)S(1)} %copy-done.24), channel_id=1, source_target_pairs={{8,16},{10,18},{12,20},{14,22},{9,17},{11,19},{13,21},{15,23}} | collective-permute-start | bytes 4718600 | tf_op jit(solution)/shard_map/cond/branch_0_fun/ppermute | solution.py:316
  129.8 60.3 %collective-permute-start.21 = (bf16[192,8,512]{2,1,0:T(8,128)(2,1)}, bf16[192,8,512]{2,1,0:T(8,128)(2,1)}, u32[]{:S(2)}, u32[]{:S(2)}) collective-permute-start(bf16[192,8,512]{2,1,0:T(8,128)(2,1)} %collective-permute-done.refs_1_.refs_0_), channel_id=1, source_target_pairs={{8,16},{10,18},{12,20},{14,22},{9,17},{11,19},{13,21},{15,23}} | collective-permute-start | bytes 4718600 | tf_op jit(solution)/shard_map/cond/branch_0_fun/ppermute | solution.py:316
  131.6 60.3 %collective-permute-start.22 = (bf16[192,8,512]{2,1,0:T(8,128)(2,1)}, bf16[192,8,512]{2,1,0:T(8,128)(2,1)}, u32[]{:S(2)}, u32[]{:S(2)}) collective-permute-start(bf16[192,8,512]{2,1,0:T(8,128)(2,1)} %collective-permute-done.1.refs_3_.refs_1_), channel_id=1, source_target_pairs={{16,8},{18,10},{20,12},{22,14},{17,9},{19,11},{21,13},{23,15}} | collective-permute-start | bytes 4718600 | tf_op jit(solution)/shard_map/cond/branch_0_fun/ppermute | solution.py:316
  133.5 30.9 %collective-permute-start.13 = (bf16[144,8,512]{2,1,0:T(8,128)(2,1)}, bf16[144,8,512]{2,1,0:T(8,128)(2,1)S(1)}, u32[]{:S(2)}, u32[]{:S(2)}) collective-permute-start(bf16[144,8,512]{2,1,0:T(8,128)(2,1)} %get-tuple-element.44), channel_id=1, source_target_pairs={{8,0},{10,2},{12,4},{14,6},{9,1},{11,3},{13,5},{15,7}} | collective-permute-start | bytes 3538952 | tf_op jit(solution)/shard_map/cond/branch_0_fun/ppermute | solution.py:316
  134.8 50.2 %collective-permute-start.14 = (bf16[144,8,512]{2,1,0:T(8,128)(2,1)}, bf16[144,8,512]{2,1,0:T(8,128)(2,1)}, u32[]{:S(2)}, u32[]{:S(2)}) collective-permute-start(bf16[144,8,512]{2,1,0:T(8,128)(2,1)} %get-tuple-element.60), channel_id=1, source_target_pairs={{8,0},{10,2},{12,4},{14,6},{9,1},{11,3},{13,5},{15,7}} | collective-permute-start | bytes 3538952 | tf_op jit(solution)/shard_map/cond/branch_0_fun/ppermute | solution.py:316
  136.1 62.6 %collective-permute-start.10 = (bf16[96,8,512]{2,1,0:T(8,128)(2,1)}, bf16[96,8,512]{2,1,0:T(8,128)(2,1)}, u32[]{:S(2)}, u32[]{:S(2)}) collective-permute-start(bf16[96,8,512]{2,1,0:T(8,128)(2,1)} %get-tuple-element.40), channel_id=1, source_target_pairs={{0,6},{2,4},{4,2},{6,0},{8,14},{10,12},{12,10},{14,8},{16,22},{18,... | collective-permute-start | bytes 2359304 | tf_op jit(solution)/shard_map/cond/branch_0_fun/ppermute | solution.py:321
  164.4 38.0 %collective-permute-start.17 = (bf16[96,8,512]{2,1,0:T(8,128)(2,1)}, bf16[96,8,512]{2,1,0:T(8,128)(2,1)S(1)}, u32[]{:S(2)}, u32[]{:S(2)}) collective-permute-start(bf16[96,8,512]{2,1,0:T(8,128)(2,1)} %get-tuple-element.54), channel_id=1, source_target_pairs={{0,2},{2,0},{4,6},{6,4},{8,10},{10,8},{12,14},{14,12},{16,18},{18,... | collective-permute-start | bytes 2359304 | tf_op jit(solution)/shard_map/cond/branch_0_fun/ppermute | solution.py:321
  191.9 31.0 %collective-permute-start.26 = (bf16[144,8,512]{2,1,0:T(8,128)(2,1)}, bf16[144,8,512]{2,1,0:T(8,128)(2,1)}, u32[]{:S(2)}, u32[]{:S(2)}) collective-permute-start(bf16[144,8,512]{2,1,0:T(8,128)(2,1)} %get-tuple-element.66), channel_id=1, source_target_pairs={{8,0},{10,2},{12,4},{14,6},{9,1},{11,3},{13,5},{15,7}} | collective-permute-start | bytes 3538952 | tf_op jit(solution)/shard_map/cond/branch_0_fun/ppermute | solution.py:316
  202.4 37.2 %collective-permute-start.23 = (bf16[144,8,512]{2,1,0:T(8,128)(2,1)}, bf16[144,8,512]{2,1,0:T(8,128)(2,1)}, u32[]{:S(2)}, u32[]{:S(2)}) collective-permute-start(bf16[144,8,512]{2,1,0:T(8,128)(2,1)} %get-tuple-element.82), channel_id=1, source_target_pairs={{16,24},{18,26},{20,28},{22,30},{17,25},{19,27},{21,29},{23,31}} | collective-permute-start | bytes 3538952 | tf_op jit(solution)/shard_map/cond/branch_0_fun/ppermute | solution.py:316
  204.1 38.1 %collective-permute-start.24 = (bf16[144,8,512]{2,1,0:T(8,128)(2,1)}, bf16[144,8,512]{2,1,0:T(8,128)(2,1)}, u32[]{:S(2)}, u32[]{:S(2)}) collective-permute-start(bf16[144,8,512]{2,1,0:T(8,128)(2,1)} %get-tuple-element.83), channel_id=1, source_target_pairs={{8,0},{10,2},{12,4},{14,6},{9,1},{11,3},{13,5},{15,7}} | collective-permute-start | bytes 3538952 | tf_op jit(solution)/shard_map/cond/branch_0_fun/ppermute | solution.py:316
  222.9 33.2 %collective-permute-start.29 = (bf16[96,8,512]{2,1,0:T(8,128)(2,1)}, bf16[96,8,512]{2,1,0:T(8,128)(2,1)}, u32[]{:S(2)}, u32[]{:S(2)}) collective-permute-start(bf16[96,8,512]{2,1,0:T(8,128)(2,1)} %get-tuple-element.78), channel_id=1, source_target_pairs={{0,6},{2,4},{4,2},{6,0},{8,14},{10,12},{12,10},{14,8},{16,22},{18,... | collective-permute-start | bytes 2359304 | tf_op jit(solution)/shard_map/cond/branch_0_fun/ppermute | solution.py:321
  247.2 55.5 %collective-permute-start.20 = (f32[384,1024]{1,0:T(8,128)}, f32[384,1024]{1,0:T(8,128)}, u32[]{:S(2)}, u32[]{:S(2)}) collective-permute-start(f32[384,1024]{1,0:T(8,128)} %dynamic-slice_bitcast_fusion), channel_id=1, source_target_pairs={{0,1},{1,0},{2,3},{3,2},{4,5},{5,4},{6,7},{7,6},{8,9},{9,8},{10,11... | collective-permute-start | bytes 4718600 | tf_op jit(solution)/shard_map/cond/branch_0_fun/ppermute | solution.py:370
  248.7 29.8 %collective-permute-start.32 = (bf16[48,8,512]{2,1,0:T(8,128)(2,1)}, bf16[48,8,512]{2,1,0:T(8,128)(2,1)}, u32[]{:S(2)}, u32[]{:S(2)}) collective-permute-start(bf16[48,8,512]{2,1,0:T(8,128)(2,1)} %get-tuple-element.91), channel_id=1, source_target_pairs={{0,6},{2,4},{4,2},{6,0},{8,14},{10,12},{12,10},{14,8},{16,22},{18,... | collective-permute-start | bytes 1179656 | tf_op jit(solution)/shard_map/cond/branch_0_fun/ppermute | solution.py:321
  256.1 32.0 %collective-permute-start.33 = (bf16[48,8,512]{2,1,0:T(8,128)(2,1)}, bf16[48,8,512]{2,1,0:T(8,128)(2,1)}, u32[]{:S(2)}, u32[]{:S(2)}) collective-permute-start(bf16[48,8,512]{2,1,0:T(8,128)(2,1)} %get-tuple-element.97), channel_id=1, source_target_pairs={{0,2},{2,0},{4,6},{6,4},{8,10},{10,8},{12,14},{14,12},{16,18},{18,... | collective-permute-start | bytes 1179656 | tf_op jit(solution)/shard_map/cond/branch_0_fun/ppermute | solution.py:321
  257.1 31.0 %collective-permute-start.34 = (bf16[48,8,512]{2,1,0:T(8,128)(2,1)}, bf16[48,8,512]{2,1,0:T(8,128)(2,1)}, u32[]{:S(2)}, u32[]{:S(2)}) collective-permute-start(bf16[48,8,512]{2,1,0:T(8,128)(2,1)} %get-tuple-element.98), channel_id=1, source_target_pairs={{0,4},{2,6},{4,0},{6,2},{8,12},{10,14},{12,8},{14,10},{16,20},{18,... | collective-permute-start | bytes 1179656 | tf_op jit(solution)/shard_map/cond/branch_0_fun/ppermute | solution.py:321
  (30 other events, 719.3 us)

commit v2 on v1

--- a/solution.py
+++ b/solution.py
@@ -13,21 +13,22 @@
 SUB = 8
 
 
-def turn(history, chunks):
+def turn(history, widths):
     rows, columns = history.shape
-    width = rows // chunks
     tile = 384 if columns % 384 == 0 else columns
 
     def kernel(x_ref, *out_refs):
-        for k, out_ref in enumerate(out_refs):
-            out_ref[...] = x_ref[k * width : (k + 1) * width, :].T.astype(jnp.bfloat16)
+        row = 0
+        for width, out_ref in zip(widths, out_refs):
+            out_ref[...] = x_ref[row : row + width, :].T.astype(jnp.bfloat16)
+            row += width
 
     return pl.pallas_call(
         kernel,
         grid=(columns // tile,),
         in_specs=[pl.BlockSpec((rows, tile), lambda i: (0, i))],
-        out_specs=[pl.BlockSpec((tile, width), lambda i: (i, 0))] * chunks,
-        out_shape=[jax.ShapeDtypeStruct((columns, width), jnp.bfloat16)] * chunks,
+        out_specs=[pl.BlockSpec((tile, width), lambda i: (i, 0)) for width in widths],
+        out_shape=[jax.ShapeDtypeStruct((columns, width), jnp.bfloat16) for width in widths],
         name="turn",
     )(history)
 
@@ -98,7 +99,7 @@
 
 def advance(share_at, own, arrived, potential, leak, drive):
     trials, share = potential.shape
-    steps = own[0].shape[1]
+    steps = STEPS
 
     def kernel(at_ref, *refs):
         own_refs, in_refs = refs[: len(own)], refs[len(own) : len(own) + len(arrived)]
@@ -106,11 +107,8 @@
         membrane = potential_ref[...]
         leak_row, drive_row = leak_ref[...], drive_ref[...]
         for s in range(steps):
-            synaptic = own_refs[0][0, s]
-            for ref in own_refs[1:]:
-                synaptic += ref[0, s]
-            for ref in in_refs:
-                synaptic += ref[s].astype(jnp.float32)
+            terms = [ref[0, s] for ref in own_refs] + [ref[s].astype(jnp.float32) for ref in in_refs]
+            synaptic = sum(terms[1:], terms[0])
             membrane = membrane + leak_row * (drive_row - membrane + synaptic)
             rate_ref[s] = jnp.maximum(membrane, 0.0) + jnp.log1p(jnp.exp(-jnp.abs(membrane)))
         last_ref[...] = membrane
@@ -136,21 +134,20 @@
     )(share_at[None], *own, *arrived, potential, leak[None], drive[None])
 
 
-def collect(table, inputs, sizes, cases, length, chosen=None):
-    width = inputs[0].shape[2]
-
+def collect(table, inputs, outputs, cases, length, chosen=None):
     def kernel(table_ref, *refs):
         in_refs, out_refs, sems = refs[: len(inputs)], refs[len(inputs) : -1], refs[-1]
 
         def carry_out(case):
-            copies = [
-                pltpu.make_async_copy(
-                    in_refs[a].at[pl.ds(table_ref[entry], length)],
-                    out_refs[o].at[pl.ds(place * length, length)],
-                    sems.at[n],
+            copies = []
+            for n, (a, entry, o, place, lane) in enumerate(case):
+                to = out_refs[o].at[pl.ds(place * length, length)]
+                width = in_refs[a].shape[2]
+                if width != out_refs[o].shape[2]:
+                    to = out_refs[o].at[pl.ds(place * length, length), :, pl.ds(lane, width)]
+                copies.append(
+                    pltpu.make_async_copy(in_refs[a].at[pl.ds(table_ref[entry], length)], to, sems.at[n])
                 )
-                for n, (a, entry, o, place) in enumerate(case)
-            ]
             for copy in copies:
                 copy.start()
             for copy in copies:
@@ -162,7 +159,7 @@
             for n, case in enumerate(cases):
                 pl.when(table_ref[chosen] == n)(functools.partial(carry_out, case))
 
-    outs = [jax.ShapeDtypeStruct((n * length, SUB, width), jnp.bfloat16) for n in sizes]
+    outs = [jax.ShapeDtypeStruct((n * length, SUB, width), jnp.bfloat16) for n, width in outputs]
     return pl.pallas_call(
         kernel,
         grid_spec=pltpu.PrefetchScalarGridSpec(
@@ -178,13 +175,12 @@
     )(table, *inputs)
 
 
-def gain_group(table, entry, windows, weights, halves, depth, shares, total=None, part=None, kind=jnp.float32):
+def gain_group(table, entry, windows, weights, first_row, depth, shares, total=None, part=None, kind=jnp.float32):
     width = windows[0].shape[2]
     targets = weights.shape[2]
     share = targets // shares
     tile = 512 if share % 512 == 0 else share
     tiles = share // tile
-    length = depth // SUB
     given = total is not None
 
     def kernel(table_ref, *refs):
@@ -192,18 +188,27 @@
         refs = refs[1 if given else 0 :]
         a_refs, w_refs, out_ref = refs[:GROUP], refs[GROUP:-1], refs[-1]
         value = old_ref[0] if given else None
-        for n in range(len(halves)):
-            for j in range(GROUP):
-                a = a_refs[j][n * length : (n + 1) * length].reshape(depth, width)
-                product = jnp.dot(a, w_refs[n * GROUP + j][0], preferred_element_type=jnp.float32)
-                value = product if value is None else value + product
+        for a_ref, w_ref in zip(a_refs, w_refs):
+            product = jnp.dot(a_ref[...].reshape(depth, width), w_ref[0], preferred_element_type=jnp.float32)
+            value = product if value is None else value + product
         out_ref[0] = value.astype(out_ref.dtype)
 
     def share_of(i, t):
         return i // tiles if part is None else lax.rem(t[AT_SHARE] + part, shares)
 
-    def weight_at(half, j):
-        return lambda i, t: (t[entry + j], half, share_of(i, t) * tiles + i % tiles)
+    def place_of(i, t):
+        return share_of(i, t) if total.shape[0] == shares else 0
+
+    def weight_spec(j):
+        def column(i, t):
+            return share_of(i, t) * tiles + i % tiles
+
+        if first_row % width == 0:
+            return pl.BlockSpec((1, width, tile), lambda i, t: (t[entry + j], first_row // width, column(i, t)))
+        return pl.BlockSpec(
+            (pl.Element(1), pl.Element(width), pl.Element(tile)),
+            lambda i, t: (t[entry + j], first_row, pl.multiple_of(column(i, t) * tile, tile)),
+        )
 
     parts = shares if part is None else 1
     return pl.pallas_call(
@@ -211,17 +216,17 @@
         grid_spec=pltpu.PrefetchScalarGridSpec(
             num_scalar_prefetch=1,
             grid=(parts * tiles,),
-            in_specs=([pl.BlockSpec((1, depth, tile), lambda i, t: (share_of(i, t), 0, i % tiles))] if given else [])
+            in_specs=([pl.BlockSpec((1, depth, tile), lambda i, t: (place_of(i, t), 0, i % tiles))] if given else [])
             + [pl.BlockSpec(w.shape, lambda i, t: (0, 0, 0)) for w in windows]
-            + [pl.BlockSpec((1, width, tile), weight_at(h, j)) for h in halves for j in range(GROUP)],
+            + [weight_spec(j) for j in range(GROUP)],
             out_specs=pl.BlockSpec((1, depth, tile), lambda i, t: (i // tiles, 0, i % tiles)),
         ),
         out_shape=jax.ShapeDtypeStruct((parts, depth, share), kind),
         cost_estimate=pl.CostEstimate(
-            flops=2 * depth * width * len(halves) * GROUP * parts * share, bytes_accessed=16 << 20, transcendentals=0
+            flops=2 * depth * width * GROUP * parts * share, bytes_accessed=16 << 20, transcendentals=0
         ),
         name="gain_group",
-    )(table, *([total] if given else []), *windows, *([weights] * (GROUP * len(halves))))
+    )(table, *([total] if given else []), *windows, *([weights] * GROUP))
 
 
 LINE = 4
@@ -325,13 +330,14 @@
         return lax.optimization_barrier((later, earlier))[0]
 
     ab = range(2)
-    counts = [slot_count] * 2
+    widths = [t.shape[2] for t in turned]
+    piece = sum(widths)
     full, slots = {}, {}
     last_step = []
 
-    def gather(inputs, sizes, cases, chosen=None):
+    def gather(inputs, outputs, cases, chosen=None):
         inputs = tie(inputs, last_step) if last_step else inputs
-        outs = collect(table, inputs, sizes, cases, length, chosen)
+        outs = collect(table, inputs, outputs, cases, length, chosen)
         last_step[:] = outs
         return outs
 
@@ -340,8 +346,8 @@
             for d in (1, -1):
                 full[s, d, h] = hop(full[s - 1, d, h], s, d, False)
         outs = gather(
-            [full[s - 1, 1, h], full[s - 1, -1, h]], counts,
-            [[(f, at_slot(2 * (s - 1) + f, k), f, k) for f in ab for k in range(slot_count)]],
+            [full[s - 1, 1, h], full[s - 1, -1, h]], [(slot_count, widths[h])] * 2,
+            [[(f, at_slot(2 * (s - 1) + f, k), f, k, 0) for f in ab for k in range(slot_count)]],
         )
         for f, d in enumerate((1, -1)):
             slots[s, d, h] = hop(outs[f], s, d, True)
@@ -352,14 +358,16 @@
         buffers += [slots[o, 1, h] for h in halves] + [slots[o, -1, h] for h in halves]
         n = len(halves)
         cases = [
-            [(c * n + h, at_window(o, j), j, h) for j in range(GROUP) for h in range(n)] for c in range(4)
+            [(c * n + h, at_window(o, j), j, 0, h * widths[0]) for j in range(GROUP) for h in range(n)]
+            for c in range(4)
         ]
-        return swap(gather(buffers, [n] * GROUP, cases, AT_CASE + o))
+        outputs = [(1, sum(widths[h] for h in halves))] * GROUP
+        return swap(gather(buffers, outputs, cases, AT_CASE + o))
 
     def add(o, windows, halves, total=None, part=None, kind=jnp.float32):
         windows = [tie(windows[0], last_step)] + windows[1:]
         return gain_group(
-            table, AT_BLOCK + o * GROUP, windows, weights, halves, depth, shares, total, part, kind
+            table, AT_BLOCK + o * GROUP, windows, weights, halves[0] * widths[0], depth, shares, total, part, kind
         )
 
     share_at = table[AT_SHARE]
@@ -367,36 +375,41 @@
     came = []
 
     def send(part, k):
-        came.append(lax.ppermute(part, "tgt", [(t, (t + k) % shares) for t in range(shares)]).reshape(shape))
+        arrived = lax.ppermute(part, "tgt", [(t, (t + k) % shares) for t in range(shares)])
+        came.append(arrived.reshape(shape))
 
     outs = gather(
-        turned, counts * 2, [[(h, at_slot(f, k), 2 * h + f, k) for h in ab for f in ab for k in range(slot_count)]]
+        turned, [(slot_count, widths[h]) for h in ab for _ in ab],
+        [[(h, at_slot(f, k), 2 * h + f, k, 0) for h in ab for f in ab for k in range(slot_count)]],
     )
     for h in ab:
         for f, d in enumerate((1, -1)):
             slots[1, d, h] = hop(outs[2 * h + f], 1, d, True)
             full[1, d, h] = hop(turned[h], 1, d, False)
-    own = gather(turned, [2] * GROUP, [[(h, at_window(0, j), j, h) for j in range(GROUP) for h in ab]])
+    own = gather(
+        turned, [(1, piece)] * GROUP,
+        [[(h, at_window(0, j), j, 0, h * widths[0]) for j in range(GROUP) for h in ab]],
+    )
     own = swap(own)
     forward(2, 0)
     first = windows_of(1, ab)
     forward(2, 1)
     total = add(0, own, ab)
+    second = [windows_of(2, (0,))]
     forward(3, 0)
-    second = windows_of(2, ab)
-    early = add(1, first, ab, total)
-    for k in range(1, shares):
-        send(lax.dynamic_index_in_dim(early, (share_at + k) % shares, 0, False), k)
+    second += [windows_of(2, (1,))]
+    send(add(1, first, ab, total, 1), 1)
+    early = add(1, first, ab, total, 0)
     forward(3, 1)
     third = [windows_of(3, (0,))]
+    late = add(2, second[0], (0,))
     third += [windows_of(3, (1,))]
-    late = add(2, second, ab)
-    late = add(3, third[0], (0,), late)
-    for k in range(1, shares):
-        send(add(3, third[1], (1,), late, k, jnp.bfloat16), k)
-    late = add(3, third[1], (1,), late, 0)
+    given = add(3, third[0], (0,), add(2, second[1], (1,), late, 1), 1)
+    send(add(3, third[1], (1,), given, 1, jnp.bfloat16), 1)
+    kept = add(3, third[0], (0,), add(2, second[1], (1,), late, 0), 0)
+    kept = add(3, third[1], (1,), kept, 0)
     return advance(
-        share_at, [early.reshape((shares,) + shape)], came + [late.reshape(shape)], potential, leak, drive
+        share_at, [], came + [early.reshape(shape), kept.reshape(shape)], potential, leak, drive
     )
 
 
@@ -415,7 +428,7 @@
     share_at = lax.axis_index("tgt")
     starts = ((hist - delays[my_area][area]) * per).astype(jnp.int32)
 
-    turned = turn(history, chunks)
+    turned = turn(history, [width] * chunks)
     arrived = [
         lax.all_gather(t, "blk", axis=0, tiled=False).reshape(size, hist * per, SUB, width) for t in turned
     ]
@@ -451,7 +464,7 @@
             came.append(part.reshape(STEPS, trials, share))
         return came
 
-    if size != LINE * GROUP or piece % 256:
+    if size != LINE * GROUP or shares != 2 or piece % 128 or piece < 256:
         return tuple(
             gather_all(history, weights, delays, boundary, potential, leak, drive, size=size, shares=shares, spread=spread)
         )
@@ -460,7 +473,8 @@
     place = jnp.stack([me // GROUP, me % GROUP, share_at])
     table = plan(area_blocks, delays, place, history.shape[1] // trials, per)
     history = lax.optimization_barrier((history, table))[0]
-    turned = [t.reshape(-1, SUB, piece // 2) for t in turn(history, 2)]
+    first_width = piece * 5 // 8 // 128 * 128
+    turned = [t.reshape(-1, SUB, t.shape[1]) for t in turn(history, (first_width, piece - first_width))]
     line = functools.partial(line_of_groups, size=size, shares=shares)
     rest = (table, turned, weights, potential, leak, drive)
     if FORCE is not None:

time: 325 us -> 322 us (level)
  waiting for transfers between devices: 156 us -> 135 us
  Pallas kernels: 113 us -> 132 us
  starting transfers between devices: 46.7 us -> 50.4 us
    ppermute x20, waiting for transfers between devices: 114 us -> 89.3 us  [hop(): return lax.ppermute(x, 'blk', pairs)]
    pallas_call x6 -> x10, Pallas kernels: 61.3 us -> 78.5 us  [gain_group(): pl.pallas_call(kernel, grid_spec=pltpu.PrefetchScalarGridSpec(num_scalar_...]
    ppermute x15 -> x18, waiting for transfers between devices: 29.3 us -> 45.3 us  [swap(): lax.ppermute(windows[j], 'blk', [(b, b ^ j) for b in range(size)])]
    ppermute x2, waiting for transfers between devices: 12.9 us -> 0.01 us  [send(): lax.ppermute(part, 'tgt', [(t, (t + k) % shares) for t in range(shares)])]
    ppermute x15 -> x18, starting transfers between devices: 8.77 us -> 11.8 us  [swap(): lax.ppermute(windows[j], 'blk', [(b, b ^ j) for b in range(size)])]
    pallas_call x10 -> x11, Pallas kernels: 39.3 us -> 41.2 us  [collect(): pl.pallas_call(kernel, grid_spec=pltpu.PrefetchScalarGridSpec(num_scalar_...]
  transfers between devices with their start and end apart: 37 -> 40, of which waited for: 12 -> 11; matrix products, arithmetic and copies ran while one was open for 1% -> 0% of each run, Pallas kernels for 31% -> 37%
where the time goes in v2:
time: 322 us; the launch traced here: 321 us
  waiting for transfers between devices  135 us (42%)
  Pallas kernels  132 us (41%)
  starting transfers between devices  50.4 us (16%)
    ppermute x20, waiting for transfers between devices, hop(): return lax.ppermute(x, 'blk', pairs)  89.3 us
    pallas_call x10, Pallas kernels, gain_group(): pl.pallas_call(kernel, grid_spec=pltpu.PrefetchScalarGridSpec(num_scalar_...  78.5 us
    ppermute x18, waiting for transfers between devices, swap(): lax.ppermute(windows[j], 'blk', [(b, b ^ j) for b in range(size)])  45.3 us
    pallas_call x11, Pallas kernels, collect(): pl.pallas_call(kernel, grid_spec=pltpu.PrefetchScalarGridSpec(num_scalar_...  41.2 us
    ppermute x20, starting transfers between devices, hop(): return lax.ppermute(x, 'blk', pairs)  35.7 us
    ppermute x18, starting transfers between devices, swap(): lax.ppermute(windows[j], 'blk', [(b, b ^ j) for b in range(size)])  11.8 us
  transfers between devices with their start and end apart: 40, of which 11 were waited for; matrix products, arithmetic and copies ran while one was open for 0% of the time, Pallas kernels for 37%

profile of v2, /device:TPU:0, one launch (start us, length us, event | category | flops | bytes accessed | tf_op | source)
XLA Modules:
  0.0 321.1 jit_solution(15565997408784367406)
XLA Ops:
  3.0 5.3 %turn.1 = (bf16[1536,640]{1,0:T(8,128)(2,1)}, bf16[1536,384]{1,0:T(8,128)(2,1)}) custom-call(f32[1024,1536]{1,0:T(8,128)} %x_ref), custom_call_target="tpu_custom_call" | custom-call | tf_op jit(solution)/shard_map/turn/pallas_call | solution.py:26
  9.5 311.4 %conditional.1 = ((f32[16,24,1024]{2,1,0:T(8,128)}, f32[24,1024]{1,0:T(8,128)})) conditional(s32[]{:T(128)} %bitcast.15, (s32[62]{0:T(128)S(1)}, bf16[192,8,640]{2,1,0:T(8,128)(2,1)}, bf16[192,8,384]{2,1,0:T(8,128)(2,1)}, bf16[16,1024,2048]{2,1,0:T(8,128)(2,1)}, f32[1024]{0:T(1024)}, /*index=5*/f32[1024]{0:T(1024)}, f32[24,1024]{1,0:T(8,128)}) %tuple.47, ...), branch_computations={%region_0.1_spmd, %region_1.2_spmd} | conditional | flops 58769809408 | bytes 470583296 | solution.py:490
  9.5 5.1 %collective-permute-start.2 = (bf16[192,8,640]{2,1,0:T(8,128)(2,1)}, bf16[192,8,640]{2,1,0:T(8,128)(2,1)S(1)}, u32[]{:S(2)}, u32[]{:S(2)}) collective-permute-start(bf16[192,8,640]{2,1,0:T(8,128)(2,1)} %get-tuple-element.35.refs_0_), channel_id=1, source_target_pairs={{0,8},{2,10},{4,12},{6,14},{8,16},{10,18},{12,20},{14,22},{1,9},{3... | collective-permute-start | bytes 5898248 | tf_op jit(solution)/shard_map/cond/branch_0_fun/ppermute | solution.py:321
  16.6 5.6 %collect.22 = (bf16[144,8,640]{2,1,0:T(8,128)(2,1)}, bf16[144,8,640]{2,1,0:T(8,128)(2,1)}, bf16[144,8,384]{2,1,0:T(8,128)(2,1)}, bf16[144,8,384]{2,1,0:T(8,128)(2,1)}) custom-call(s32[62]{0:T(128)S(1)} %get-tuple-element.28.table_ref, bf16[192,8,640]{2,1,0:T(8,128)(2,1)} %get-tuple-element.35.refs_0_, bf16[192,8,384]{2,1,0:T(8,128)(2,1)} %get-tuple-element.36.refs_1_), custom_call_target="tpu_custom_call" | custom-call | flops 3000000000 | bytes 6291456 | tf_op jit(solution)/shard_map/cond/branch_0_fun/collect/pallas_call | solution.py:163
  29.8 28.2 %collective-permute-done.2.refs_0_ = bf16[192,8,640]{2,1,0:T(8,128)(2,1)S(1)} collective-permute-done((bf16[192,8,640]{2,1,0:T(8,128)(2,1)}, bf16[192,8,640]{2,1,0:T(8,128)(2,1)S(1)}, u32[]{:S(2)}, u32[]{:S(2)}) %collective-permute-start.2) | collective-permute-done | bytes 1966112 | tf_op jit(solution)/shard_map/cond/branch_0_fun/ppermute | solution.py:321
  60.6 4.3 %collect.23 = (bf16[48,8,1024]{2,1,0:T(8,128)(2,1)}, bf16[48,8,1024]{2,1,0:T(8,128)(2,1)}, bf16[48,8,1024]{2,1,0:T(8,128)(2,1)}, bf16[48,8,1024]{2,1,0:T(8,128)(2,1)}) custom-call(s32[62]{0:T(128)S(1)} %get-tuple-element.28.table_ref, bf16[192,8,640]{2,1,0:T(8,128)(2,1)} %get-tuple-element.35.refs_0_, bf16[192,8,384]{2,1,0:T(8,128)(2,1)} %get-tuple-element.36.refs_1_), custom_call_target="tpu_custom_call" | custom-call | flops 3000000000 | bytes 6291456 | tf_op jit(solution)/shard_map/cond/branch_0_fun/collect/pallas_call | solution.py:163
  69.0 13.8 %collective-permute-done.7.refs_7_ = bf16[144,8,384]{2,1,0:T(8,128)(2,1)} collective-permute-done((bf16[144,8,384]{2,1,0:T(8,128)(2,1)}, bf16[144,8,384]{2,1,0:T(8,128)(2,1)}, u32[]{:S(2)}, u32[]{:S(2)}) %collective-permute-start.7) | collective-permute-done | bytes 884768 | tf_op jit(solution)/shard_map/cond/branch_0_fun/ppermute | solution.py:321
  88.6 25.7 %collective-permute-done.6.refs_6_ = bf16[144,8,640]{2,1,0:T(8,128)(2,1)} collective-permute-done((bf16[144,8,640]{2,1,0:T(8,128)(2,1)}, bf16[144,8,640]{2,1,0:T(8,128)(2,1)}, u32[]{:S(2)}, u32[]{:S(2)}) %collective-permute-start.6) | collective-permute-done | bytes 1474592 | tf_op jit(solution)/shard_map/cond/branch_0_fun/ppermute | solution.py:321
  114.3 20.0 %collective-permute-done.10.refs_3_ = bf16[48,8,1024]{2,1,0:T(8,128)(2,1)S(1)} collective-permute-done((bf16[48,8,1024]{2,1,0:T(8,128)(2,1)}, bf16[48,8,1024]{2,1,0:T(8,128)(2,1)S(1)}, u32[]{:S(2)}, u32[]{:S(2)}) %collective-permute-start.10) | collective-permute-done | bytes 786464 | tf_op jit(solution)/shard_map/cond/branch_0_fun/ppermute | solution.py:326
  160.7 11.4 %collective-permute-done.12.refs_3_ = bf16[144,8,384]{2,1,0:T(8,128)(2,1)} collective-permute-done((bf16[144,8,384]{2,1,0:T(8,128)(2,1)}, bf16[144,8,384]{2,1,0:T(8,128)(2,1)}, u32[]{:S(2)}, u32[]{:S(2)}) %collective-permute-start.12) | collective-permute-done | bytes 884768 | tf_op jit(solution)/shard_map/cond/branch_0_fun/ppermute | solution.py:321
  182.1 7.9 %collective-permute-done.18.refs_3_ = bf16[48,8,1024]{2,1,0:T(8,128)(2,1)S(1)} collective-permute-done((bf16[48,8,1024]{2,1,0:T(8,128)(2,1)}, bf16[48,8,1024]{2,1,0:T(8,128)(2,1)S(1)}, u32[]{:S(2)}, u32[]{:S(2)}) %collective-permute-start.18) | collective-permute-done | bytes 786464 | tf_op jit(solution)/shard_map/cond/branch_0_fun/ppermute | solution.py:326
  191.5 13.0 %gain_group.20.refs_0_ = f32[2,384,1024]{2,1,0:T(8,128)} custom-call(s32[62]{0:T(128)S(1)} %get-tuple-element.28.table_ref, bf16[48,8,1024]{2,1,0:T(8,128)(2,1)} %get-tuple-element.61.refs_0_, bf16[48,8,1024]{2,1,0:T(8,128)(2,1)} %copy-done.21, bf16[48,8,1024]{2,1,0:T(8,128)(2,1)} %collective-permute-done.9.refs_2_, bf16[48,8,1024]{2,1,0:T(8,128)(2,1)} %copy-done.20, ...), custom_call_target="tpu_custom_call" | custom-call | flops 6442450944 | bytes 16777216 | tf_op jit(solution)/shard_map/cond/branch_0_fun/gain_group/pallas_call | solution.py:214
  208.2 9.1 %gain_group.21 = f32[1,384,1024]{2,1,0:T(8,128)} custom-call(s32[62]{0:T(128)S(1)} %get-tuple-element.28.table_ref, f32[2,384,1024]{2,1,0:T(8,128)} %gain_group.20.refs_0_, bf16[48,8,1024]{2,1,0:T(8,128)(2,1)} %get-tuple-element.83.refs_1_, bf16[48,8,1024]{2,1,0:T(8,128)(2,1)} %copy-done, bf16[48,8,1024]{2,1,0:T(8,128)(2,1)} %copy-done.1, ...), custom_call_target="tpu_custom_call" | custom-call | flops 3221225472 | bytes 16777216 | tf_op jit(solution)/shard_map/cond/branch_0_fun/gain_group/pallas_call | solution.py:214
  218.0 9.2 %collective-permute-done.29.refs_3_ = bf16[144,8,384]{2,1,0:T(8,128)(2,1)} collective-permute-done((bf16[144,8,384]{2,1,0:T(8,128)(2,1)}, bf16[144,8,384]{2,1,0:T(8,128)(2,1)}, u32[]{:S(2)}, u32[]{:S(2)}) %collective-permute-start.29) | collective-permute-done | bytes 884768 | tf_op jit(solution)/shard_map/cond/branch_0_fun/ppermute | solution.py:321
  239.1 10.4 %gain_group.22.refs_0_ = f32[2,384,1024]{2,1,0:T(8,128)} custom-call(s32[62]{0:T(128)S(1)} %get-tuple-element.28.table_ref, bf16[48,8,640]{2,1,0:T(8,128)(2,1)} %get-tuple-element.96.refs_0_, bf16[48,8,640]{2,1,0:T(8,128)(2,1)} %copy-done.24, bf16[48,8,640]{2,1,0:T(8,128)(2,1)} %copy-done.25, bf16[48,8,640]{2,1,0:T(8,128)(2,1)} %copy-done.26, ...), custom_call_target="tpu_custom_call" | custom-call | flops 4026531840 | bytes 16777216 | tf_op jit(solution)/shard_map/cond/branch_0_fun/gain_group/pallas_call | solution.py:214
  249.5 15.3 %collective-permute-done.32.refs_4_ = bf16[48,8,384]{2,1,0:T(8,128)(2,1)S(1)} collective-permute-done((bf16[48,8,384]{2,1,0:T(8,128)(2,1)}, bf16[48,8,384]{2,1,0:T(8,128)(2,1)S(1)}, u32[]{:S(2)}, u32[]{:S(2)}) %collective-permute-start.32) | collective-permute-done | bytes 294944 | tf_op jit(solution)/shard_map/cond/branch_0_fun/ppermute | solution.py:326
  266.7 5.5 %gain_group.23.refs_0_ = f32[1,384,1024]{2,1,0:T(8,128)} custom-call(s32[62]{0:T(128)S(1)} %get-tuple-element.28.table_ref, f32[2,384,1024]{2,1,0:T(8,128)} %gain_group.22.refs_0_, bf16[48,8,384]{2,1,0:T(8,128)(2,1)} %get-tuple-element.105.refs_1_, bf16[48,8,384]{2,1,0:T(8,128)(2,1)} %copy-done.14, bf16[48,8,384]{2,1,0:T(8,128)(2,1)} %copy-done.15, ...), custom_call_target="tpu_custom_call" | custom-call | flops 1207959552 | bytes 16777216 | tf_op jit(solution)/shard_map/cond/branch_0_fun/gain_group/pallas_call | solution.py:214
  272.2 7.4 %gain_group.24.refs_0_ = f32[1,384,1024]{2,1,0:T(8,128)} custom-call(s32[62]{0:T(128)S(1)} %get-tuple-element.28.table_ref, f32[1,384,1024]{2,1,0:T(8,128)} %gain_group.23.refs_0_, bf16[48,8,640]{2,1,0:T(8,128)(2,1)} %get-tuple-element.106.refs_1_, bf16[48,8,640]{2,1,0:T(8,128)(2,1)} %copy-done.6, bf16[48,8,640]{2,1,0:T(8,128)(2,1)} %copy-done.8, ...), custom_call_target="tpu_custom_call" | custom-call | flops 2013265920 | bytes 16777216 | tf_op jit(solution)/shard_map/cond/branch_0_fun/gain_group/pallas_call | solution.py:214
  280.2 5.4 %gain_group.25 = bf16[1,384,1024]{2,1,0:T(8,128)(2,1)} custom-call(s32[62]{0:T(128)S(1)} %get-tuple-element.28.table_ref, f32[1,384,1024]{2,1,0:T(8,128)} %gain_group.24.refs_0_, bf16[48,8,384]{2,1,0:T(8,128)(2,1)} %get-tuple-element.107.refs_1_, bf16[48,8,384]{2,1,0:T(8,128)(2,1)} %collective-permute-done.36.refs_2_, ...), custom_call_target="tpu_custom_call" | custom-call | flops 1207959552 | bytes 16777216 | tf_op jit(solution)/shard_map/cond/branch_0_fun/gain_group/pallas_call | solution.py:214
  287.7 9.2 %gain_group.26 = f32[1,384,1024]{2,1,0:T(8,128)} custom-call(s32[62]{0:T(128)S(1)} %get-tuple-element.28.table_ref, f32[2,384,1024]{2,1,0:T(8,128)} %gain_group.20.refs_0_, bf16[48,8,1024]{2,1,0:T(8,128)(2,1)} %get-tuple-element.83.refs_1_, bf16[48,8,1024]{2,1,0:T(8,128)(2,1)} %copy-done, bf16[48,8,1024]{2,1,0:T(8,128)(2,1)} %copy-done.1, ...), custom_call_target="tpu_custom_call" | custom-call | flops 3221225472 | bytes 16777216 | tf_op jit(solution)/shard_map/cond/branch_0_fun/gain_group/pallas_call | solution.py:214
  296.9 5.6 %gain_group.27.refs_0_ = f32[1,384,1024]{2,1,0:T(8,128)} custom-call(s32[62]{0:T(128)S(1)} %get-tuple-element.28.table_ref, f32[2,384,1024]{2,1,0:T(8,128)} %gain_group.22.refs_0_, bf16[48,8,384]{2,1,0:T(8,128)(2,1)} %get-tuple-element.105.refs_1_, bf16[48,8,384]{2,1,0:T(8,128)(2,1)} %copy-done.14, bf16[48,8,384]{2,1,0:T(8,128)(2,1)} %copy-done.15, ...), custom_call_target="tpu_custom_call" | custom-call | flops 1207959552 | bytes 16777216 | tf_op jit(solution)/shard_map/cond/branch_0_fun/gain_group/pallas_call | solution.py:214
  302.5 7.3 %gain_group.28.refs_0_ = f32[1,384,1024]{2,1,0:T(8,128)} custom-call(s32[62]{0:T(128)S(1)} %get-tuple-element.28.table_ref, f32[1,384,1024]{2,1,0:T(8,128)} %gain_group.27.refs_0_, bf16[48,8,640]{2,1,0:T(8,128)(2,1)} %get-tuple-element.106.refs_1_, bf16[48,8,640]{2,1,0:T(8,128)(2,1)} %copy-done.6, bf16[48,8,640]{2,1,0:T(8,128)(2,1)} %copy-done.8, ...), custom_call_target="tpu_custom_call" | custom-call | flops 2013265920 | bytes 16777216 | tf_op jit(solution)/shard_map/cond/branch_0_fun/gain_group/pallas_call | solution.py:214
  309.8 5.6 %gain_group.29 = f32[1,384,1024]{2,1,0:T(8,128)} custom-call(s32[62]{0:T(128)S(1)} %get-tuple-element.28.table_ref, f32[1,384,1024]{2,1,0:T(8,128)} %gain_group.28.refs_0_, bf16[48,8,384]{2,1,0:T(8,128)(2,1)} %get-tuple-element.107.refs_1_, bf16[48,8,384]{2,1,0:T(8,128)(2,1)} %collective-permute-done.36.refs_2_, ...), custom_call_target="tpu_custom_call" | custom-call | flops 1207959552 | bytes 16777216 | tf_op jit(solution)/shard_map/cond/branch_0_fun/gain_group/pallas_call | solution.py:214
  315.4 5.5 %advance.2 = (f32[16,24,1024]{2,1,0:T(8,128)}, f32[24,1024]{1,0:T(8,128)}) custom-call(s32[1]{0:T(128)} %slice.6.at_ref, f32[16,24,1024]{2,1,0:T(8,128)} %bitcast.refs_0_, bf16[16,24,1024]{2,1,0:T(8,128)(2,1)} %bitcast.1.refs_1_, f32[16,24,1024]{2,1,0:T(8,128)} %bitcast.18, f32[16,24,1024]{2,1,0:T(8,128)} %bitcast.20, f32[24,1024]{1,0:T(8,128)S(1)} %copy-done.30, ...), custom_call_target="tpu_custom_call" | custom-call | tf_op jit(solution)/shard_map/cond/branch_0_fun/advance/pallas_call | solution.py:121
  (124 shorter events, 83.4 us)
Async XLA Ops:
  9.5 48.5 %collective-permute-start.2 = (bf16[192,8,640]{2,1,0:T(8,128)(2,1)}, bf16[192,8,640]{2,1,0:T(8,128)(2,1)S(1)}, u32[]{:S(2)}, u32[]{:S(2)}) collective-permute-start(bf16[192,8,640]{2,1,0:T(8,128)(2,1)} %get-tuple-element.35.refs_0_), channel_id=1, source_target_pairs={{0,8},{2,10},{4,12},{6,14},{8,16},{10,18},{12,20},{14,22},{1,9},{3... | collective-permute-start | bytes 5898248 | tf_op jit(solution)/shard_map/cond/branch_0_fun/ppermute | solution.py:321
  14.6 44.7 %collective-permute-start.3 = (bf16[192,8,640]{2,1,0:T(8,128)(2,1)}, bf16[192,8,640]{2,1,0:T(8,128)(2,1)}, u32[]{:S(2)}, u32[]{:S(2)}) collective-permute-start(bf16[192,8,640]{2,1,0:T(8,128)(2,1)} %get-tuple-element.35.refs_0_), channel_id=1, source_target_pairs={{16,8},{18,10},{20,12},{22,14},{24,16},{26,18},{28,20},{30,22},{17... | collective-permute-start | bytes 5898248 | tf_op jit(solution)/shard_map/cond/branch_0_fun/ppermute | solution.py:321
  22.9 63.7 %collective-permute-start.4 = (bf16[144,8,640]{2,1,0:T(8,128)(2,1)}, bf16[144,8,640]{2,1,0:T(8,128)(2,1)}, u32[]{:S(2)}, u32[]{:S(2)}) collective-permute-start(bf16[144,8,640]{2,1,0:T(8,128)(2,1)} %get-tuple-element.31), channel_id=1, source_target_pairs={{16,24},{18,26},{20,28},{22,30},{17,25},{19,27},{21,29},{23,31}} | collective-permute-start | bytes 4423688 | tf_op jit(solution)/shard_map/cond/branch_0_fun/ppermute | solution.py:321
  24.7 59.8 %collective-permute-start = (bf16[192,8,384]{2,1,0:T(8,128)(2,1)}, bf16[192,8,384]{2,1,0:T(8,128)(2,1)}, u32[]{:S(2)}, u32[]{:S(2)}) collective-permute-start(bf16[192,8,384]{2,1,0:T(8,128)(2,1)} %get-tuple-element.36.refs_1_), channel_id=1, source_target_pairs={{0,8},{2,10},{4,12},{6,14},{8,16},{10,18},{12,20},{14,22},{1,9},{3... | collective-permute-start | bytes 3538952 | tf_op jit(solution)/shard_map/cond/branch_0_fun/ppermute | solution.py:321
  28.2 57.1 %collective-permute-start.1 = (bf16[192,8,384]{2,1,0:T(8,128)(2,1)}, bf16[192,8,384]{2,1,0:T(8,128)(2,1)}, u32[]{:S(2)}, u32[]{:S(2)}) collective-permute-start(bf16[192,8,384]{2,1,0:T(8,128)(2,1)} %get-tuple-element.36.refs_1_), channel_id=1, source_target_pairs={{16,8},{18,10},{20,12},{22,14},{24,16},{26,18},{28,20},{30,22},{17... | collective-permute-start | bytes 3538952 | tf_op jit(solution)/shard_map/cond/branch_0_fun/ppermute | solution.py:321
  59.3 55.0 %collective-permute-start.6 = (bf16[144,8,640]{2,1,0:T(8,128)(2,1)}, bf16[144,8,640]{2,1,0:T(8,128)(2,1)}, u32[]{:S(2)}, u32[]{:S(2)}) collective-permute-start(bf16[144,8,640]{2,1,0:T(8,128)(2,1)} %get-tuple-element.32), channel_id=1, source_target_pairs={{8,0},{10,2},{12,4},{14,6},{9,1},{11,3},{13,5},{15,7}} | collective-permute-start | bytes 4423688 | tf_op jit(solution)/shard_map/cond/branch_0_fun/ppermute | solution.py:321
  82.7 53.3 %collective-permute-start.15 = (bf16[144,8,640]{2,1,0:T(8,128)(2,1)}, bf16[144,8,640]{2,1,0:T(8,128)(2,1)}, u32[]{:S(2)}, u32[]{:S(2)}) collective-permute-start(bf16[144,8,640]{2,1,0:T(8,128)(2,1)} %get-tuple-element.43), channel_id=1, source_target_pairs={{16,24},{18,26},{20,28},{22,30},{17,25},{19,27},{21,29},{23,31}} | collective-permute-start | bytes 4423688 | tf_op jit(solution)/shard_map/cond/branch_0_fun/ppermute | solution.py:321
  84.5 61.7 %collective-permute-start.13 = (bf16[192,8,640]{2,1,0:T(8,128)(2,1)}, bf16[192,8,640]{2,1,0:T(8,128)(2,1)S(1)}, u32[]{:S(2)}, u32[]{:S(2)}) collective-permute-start(bf16[192,8,640]{2,1,0:T(8,128)(2,1)} %copy-done.37), channel_id=1, source_target_pairs={{8,16},{10,18},{12,20},{14,22},{9,17},{11,19},{13,21},{15,23}} | collective-permute-start | bytes 5898248 | tf_op jit(solution)/shard_map/cond/branch_0_fun/ppermute | solution.py:321
  85.3 57.6 %collective-permute-start.16 = (bf16[144,8,640]{2,1,0:T(8,128)(2,1)}, bf16[144,8,640]{2,1,0:T(8,128)(2,1)}, u32[]{:S(2)}, u32[]{:S(2)}) collective-permute-start(bf16[144,8,640]{2,1,0:T(8,128)(2,1)} %get-tuple-element.44), channel_id=1, source_target_pairs={{8,0},{10,2},{12,4},{14,6},{9,1},{11,3},{13,5},{15,7}} | collective-permute-start | bytes 4423688 | tf_op jit(solution)/shard_map/cond/branch_0_fun/ppermute | solution.py:321
  86.6 61.2 %collective-permute-start.14 = (bf16[192,8,640]{2,1,0:T(8,128)(2,1)}, bf16[192,8,640]{2,1,0:T(8,128)(2,1)}, u32[]{:S(2)}, u32[]{:S(2)}) collective-permute-start(bf16[192,8,640]{2,1,0:T(8,128)(2,1)} %collective-permute-done.3.refs_1_.refs_2_), channel_id=1, source_target_pairs={{16,8},{18,10},{20,12},{22,14},{17,9},{19,11},{21,13},{23,15}} | collective-permute-start | bytes 5898248 | tf_op jit(solution)/shard_map/cond/branch_0_fun/ppermute | solution.py:321
  158.2 48.5 %collective-permute-start.21 = (bf16[144,8,640]{2,1,0:T(8,128)(2,1)}, bf16[144,8,640]{2,1,0:T(8,128)(2,1)}, u32[]{:S(2)}, u32[]{:S(2)}) collective-permute-start(bf16[144,8,640]{2,1,0:T(8,128)(2,1)} %get-tuple-element.73), channel_id=1, source_target_pairs={{16,24},{18,26},{20,28},{22,30},{17,25},{19,27},{21,29},{23,31}} | collective-permute-start | bytes 4423688 | tf_op jit(solution)/shard_map/cond/branch_0_fun/ppermute | solution.py:321
  160.3 29.8 %collective-permute-start.18 = (bf16[48,8,1024]{2,1,0:T(8,128)(2,1)}, bf16[48,8,1024]{2,1,0:T(8,128)(2,1)S(1)}, u32[]{:S(2)}, u32[]{:S(2)}) collective-permute-start(bf16[48,8,1024]{2,1,0:T(8,128)(2,1)} %get-tuple-element.55), channel_id=1, source_target_pairs={{0,4},{2,6},{4,0},{6,2},{8,12},{10,14},{12,8},{14,10},{16,20},{18,... | collective-permute-start | bytes 2359304 | tf_op jit(solution)/shard_map/cond/branch_0_fun/ppermute | solution.py:326
  172.1 45.3 %collective-permute-start.22 = (bf16[144,8,640]{2,1,0:T(8,128)(2,1)}, bf16[144,8,640]{2,1,0:T(8,128)(2,1)}, u32[]{:S(2)}, u32[]{:S(2)}) collective-permute-start(bf16[144,8,640]{2,1,0:T(8,128)(2,1)} %get-tuple-element.74), channel_id=1, source_target_pairs={{8,0},{10,2},{12,4},{14,6},{9,1},{11,3},{13,5},{15,7}} | collective-permute-start | bytes 4423688 | tf_op jit(solution)/shard_map/cond/branch_0_fun/ppermute | solution.py:321
  176.4 29.6 %collective-permute-start.19 = (bf16[48,8,1024]{2,1,0:T(8,128)(2,1)S(1)}, bf16[48,8,1024]{2,1,0:T(8,128)(2,1)S(1)}, u32[]{:S(2)}, u32[]{:S(2)}) collective-permute-start(bf16[48,8,1024]{2,1,0:T(8,128)(2,1)S(1)} %copy-done.40), channel_id=1, source_target_pairs={{0,6},{2,4},{4,2},{6,0},{8,14},{10,12},{12,10},{14,8},{16,22},{18,... | collective-permute-start | bytes 2359304 | tf_op jit(solution)/shard_map/cond/branch_0_fun/ppermute | solution.py:326
  180.6 37.3 %collective-permute-start.28 = (bf16[144,8,384]{2,1,0:T(8,128)(2,1)}, bf16[144,8,384]{2,1,0:T(8,128)(2,1)}, u32[]{:S(2)}, u32[]{:S(2)}) collective-permute-start(bf16[144,8,384]{2,1,0:T(8,128)(2,1)} %get-tuple-element.86), channel_id=1, source_target_pairs={{16,24},{18,26},{20,28},{22,30},{17,25},{19,27},{21,29},{23,31}} | collective-permute-start | bytes 2654216 | tf_op jit(solution)/shard_map/cond/branch_0_fun/ppermute | solution.py:321
  190.1 37.1 %collective-permute-start.29 = (bf16[144,8,384]{2,1,0:T(8,128)(2,1)}, bf16[144,8,384]{2,1,0:T(8,128)(2,1)}, u32[]{:S(2)}, u32[]{:S(2)}) collective-permute-start(bf16[144,8,384]{2,1,0:T(8,128)(2,1)} %get-tuple-element.87), channel_id=1, source_target_pairs={{8,0},{10,2},{12,4},{14,6},{9,1},{11,3},{13,5},{15,7}} | collective-permute-start | bytes 2654216 | tf_op jit(solution)/shard_map/cond/branch_0_fun/ppermute | solution.py:321
  206.0 26.1 %collective-permute-start.25 = (bf16[48,8,640]{2,1,0:T(8,128)(2,1)}, bf16[48,8,640]{2,1,0:T(8,128)(2,1)S(1)}, u32[]{:S(2)}, u32[]{:S(2)}) collective-permute-start(bf16[48,8,640]{2,1,0:T(8,128)(2,1)} %get-tuple-element.68), channel_id=1, source_target_pairs={{0,2},{2,0},{4,6},{6,4},{8,10},{10,8},{12,14},{14,12},{16,18},{18,... | collective-permute-start | bytes 1474568 | tf_op jit(solution)/shard_map/cond/branch_0_fun/ppermute | solution.py:326
  206.7 25.5 %collective-permute-start.26 = (bf16[48,8,640]{2,1,0:T(8,128)(2,1)}, bf16[48,8,640]{2,1,0:T(8,128)(2,1)S(1)}, u32[]{:S(2)}, u32[]{:S(2)}) collective-permute-start(bf16[48,8,640]{2,1,0:T(8,128)(2,1)} %get-tuple-element.69), channel_id=1, source_target_pairs={{0,4},{2,6},{4,0},{6,2},{8,12},{10,14},{12,8},{14,10},{16,20},{18,... | collective-permute-start | bytes 1474568 | tf_op jit(solution)/shard_map/cond/branch_0_fun/ppermute | solution.py:326
  232.1 32.9 %collective-permute-start.33 = (bf16[48,8,640]{2,1,0:T(8,128)(2,1)}, bf16[48,8,640]{2,1,0:T(8,128)(2,1)S(1)}, u32[]{:S(2)}, u32[]{:S(2)}) collective-permute-start(bf16[48,8,640]{2,1,0:T(8,128)(2,1)} %get-tuple-element.93), channel_id=1, source_target_pairs={{0,2},{2,0},{4,6},{6,4},{8,10},{10,8},{12,14},{14,12},{16,18},{18,... | collective-permute-start | bytes 1474568 | tf_op jit(solution)/shard_map/cond/branch_0_fun/ppermute | solution.py:326
  232.2 33.8 %collective-permute-start.34 = (bf16[48,8,640]{2,1,0:T(8,128)(2,1)}, bf16[48,8,640]{2,1,0:T(8,128)(2,1)S(1)}, u32[]{:S(2)}, u32[]{:S(2)}) collective-permute-start(bf16[48,8,640]{2,1,0:T(8,128)(2,1)} %get-tuple-element.94), channel_id=1, source_target_pairs={{0,4},{2,6},{4,0},{6,2},{8,12},{10,14},{12,8},{14,10},{16,20},{18,... | collective-permute-start | bytes 1474568 | tf_op jit(solution)/shard_map/cond/branch_0_fun/ppermute | solution.py:326
  235.7 36.5 %collective-permute-start.35 = (bf16[48,8,640]{2,1,0:T(8,128)(2,1)}, bf16[48,8,640]{2,1,0:T(8,128)(2,1)}, u32[]{:S(2)}, u32[]{:S(2)}) collective-permute-start(bf16[48,8,640]{2,1,0:T(8,128)(2,1)} %get-tuple-element.95), channel_id=1, source_target_pairs={{0,6},{2,4},{4,2},{6,0},{8,14},{10,12},{12,10},{14,8},{16,22},{18,... | collective-permute-start | bytes 1474568 | tf_op jit(solution)/shard_map/cond/branch_0_fun/ppermute | solution.py:326
  237.1 27.7 %collective-permute-start.32 = (bf16[48,8,384]{2,1,0:T(8,128)(2,1)}, bf16[48,8,384]{2,1,0:T(8,128)(2,1)S(1)}, u32[]{:S(2)}, u32[]{:S(2)}) collective-permute-start(bf16[48,8,384]{2,1,0:T(8,128)(2,1)} %get-tuple-element.82), channel_id=1, source_target_pairs={{0,6},{2,4},{4,2},{6,0},{8,14},{10,12},{12,10},{14,8},{16,22},{18,... | collective-permute-start | bytes 884744 | tf_op jit(solution)/shard_map/cond/branch_0_fun/ppermute | solution.py:326
  237.6 77.8 %collective-permute-start.20 = (f32[1,384,1024]{2,1,0:T(8,128)}, f32[1,384,1024]{2,1,0:T(8,128)}, u32[]{:S(2)}, u32[]{:S(2)}) collective-permute-start(f32[1,384,1024]{2,1,0:T(8,128)} %gain_group.21), channel_id=1, source_target_pairs={{0,1},{1,0},{2,3},{3,2},{4,5},{5,4},{6,7},{7,6},{8,9},{9,8},{10,11... | collective-permute-start | bytes 4718600 | tf_op jit(solution)/shard_map/cond/branch_0_fun/ppermute | solution.py:378
  285.6 29.7 %collective-permute-start.39 = (bf16[1,384,1024]{2,1,0:T(8,128)(2,1)}, bf16[1,384,1024]{2,1,0:T(8,128)(2,1)}, u32[]{:S(2)}, u32[]{:S(2)}) collective-permute-start(bf16[1,384,1024]{2,1,0:T(8,128)(2,1)} %gain_group.25), channel_id=1, source_target_pairs={{0,1},{1,0},{2,3},{3,2},{4,5},{5,4},{6,7},{7,6},{8,9},{9,8},{10,11... | collective-permute-start | bytes 2359304 | tf_op jit(solution)/shard_map/cond/branch_0_fun/ppermute | solution.py:378
  (36 other events, 457.3 us)
